TPU v7x, 32 devices: a whole 2x2x4 slice. The times are simulated.
32 devices in a mesh: seq: 8 (over z, y), tp: 4 (over x, core).
Axes of the slice: x: 2, y: 2, z: 4, core: 2. Of those that a mesh axis runs over, the one named last changes fastest.
Arguments:
- tokens: bfloat16 [6144, 4096], P('seq'), may hold values from -6 to 6
- query_weight: bfloat16 [4096, 2048], P('seq', 'tp'), may hold values from -0.09375 to 0.09375
- key_weight: bfloat16 [4096, 2048], P('seq', 'tp'), may hold values from -0.09375 to 0.09375
- value_weight: bfloat16 [4096, 2048], P('seq', 'tp'), may hold values from -0.09375 to 0.09375
- gate_weight: bfloat16 [4096, 16], P('seq', 'tp'), may hold values from -0.09375 to 0.09375
- decay_rate: float32 [16], P('tp'), may hold values from 3.2552085e-05 to 0.04
- norm_gain: float32 [2048], P('tp'), may hold values from 0.5 to 1.5
- out_weight: bfloat16 [2048, 4096], P(None, 'tp'), may hold values from -0.125 to 0.125
Outputs:
- mixed: bfloat16 [6144, 4096], P('seq', 'tp')
All inputs are finite; a program needn't handle non-finite values.
Results may differ from a plain program's by a relative error of at most 0.006.
The roundings to bfloat16 on the way count: a program that leaves them out, or rounds other values in their place, can miss the bound.
Values may be sent and summed in bfloat16 or wider, within the bound.
No kernel may reach another device: no remote copies, remote signals or barrier semaphores. Data moves between devices by JAX's collectives and lax.ppermute only.
A program may use at most 128 MiB of HBM per device.

v0:
```python
import jax
import jax.numpy as jnp
from jax import lax
from jax.sharding import PartitionSpec as P


def on_device(
    tokens, query_weight, key_weight, value_weight, gate_weight, decay_rate, norm_gain, out_weight
):
    tok_rows = tokens.shape[0]
    head_count = decay_rate.shape[0]
    proj_width = query_weight.shape[1]
    head_size = proj_width // head_count

    def contract(piece):
        return jnp.dot(tokens, piece, preferred_element_type=jnp.float32)

    query_proj = contract(lax.all_gather(query_weight, "seq", axis=0, tiled=True))
    pieces = (
        lax.all_gather(key_weight, "seq", axis=0, tiled=True),
        lax.all_gather(value_weight, "seq", axis=0, tiled=True),
        lax.all_gather(gate_weight, "seq", axis=0, tiled=True),
    )
    key_proj, value_proj, gate_logit = tuple((contract(one_piece) for one_piece in pieces))
    query_heads = query_proj.astype(jnp.bfloat16).reshape(tok_rows, head_count, head_size)
    key_heads = key_proj.astype(jnp.bfloat16).reshape(tok_rows, head_count, head_size)
    value_per_head = value_proj.astype(jnp.bfloat16).reshape(tok_rows, head_count, head_size)
    log_decay = -decay_rate[None, :] * jax.nn.softplus(gate_logit)
    within = jnp.cumsum(log_decay, axis=0)
    block_total = within[-1]
    key_scaled = (jnp.exp(block_total[None, :] - within)[:, :, None] * key_heads).astype(
        jnp.bfloat16
    )
    shard_local_state = jnp.einsum(
        "gfw,gfz->fwz", key_scaled, value_per_head, preferred_element_type=jnp.float32
    )
    all_totals = lax.all_gather(block_total[None, :], "seq", axis=0, tiled=True)
    running_sum = jnp.cumsum(all_totals, axis=0)
    seq_rank = lax.axis_index("seq")
    before = lax.dynamic_index_in_dim(running_sum, jnp.maximum(seq_rank - 1, 0), 0, keepdims=False)
    piece = lax.all_gather(shard_local_state[None], "seq", axis=0, tiled=True)
    piece_rows = piece.shape[0]
    positions = jnp.arange(piece_rows, dtype=jnp.int32)
    earlier_ok = (positions < seq_rank)[:, None]
    factor = jnp.where(
        earlier_ok, jnp.exp(jnp.where(earlier_ok, before[None, :] - running_sum, 0.0)), 0.0
    )
    prefix_state = jnp.sum(factor[:, :, None, None] * piece, axis=0)
    query_scaled = (jnp.exp(within)[:, :, None] * query_heads).astype(jnp.bfloat16)
    carried_state = jnp.einsum(
        "fys,ysu->fyu",
        query_scaled,
        prefix_state.astype(jnp.bfloat16),
        preferred_element_type=jnp.float32,
    )
    scores = jnp.einsum("thk,shk->hts", query_heads, key_heads, preferred_element_type=jnp.float32)
    row_index = lax.broadcasted_iota(jnp.int32, (tok_rows, tok_rows), 0)
    col_index = lax.broadcasted_iota(jnp.int32, (tok_rows, tok_rows), 1)
    causal = (col_index <= row_index)[None, :, :]
    decay_gap = within.T[:, :, None] - within.T[:, None, :]
    attn = jnp.where(causal, scores * jnp.exp(jnp.where(causal, decay_gap, 0.0)), 0.0).astype(
        jnp.bfloat16
    )
    local_part = jnp.einsum(
        "hts,shv->thv", attn, value_per_head, preferred_element_type=jnp.float32
    )
    head_out = carried_state + local_part
    mean_square = jnp.mean(head_out * head_out, axis=-1, keepdims=True)
    normed = (head_out * lax.rsqrt(mean_square + 1e-05)).reshape(tok_rows, proj_width) * norm_gain[
        None, :
    ]
    normed = normed.astype(jnp.bfloat16)
    mixed = jnp.dot(
        lax.all_gather(normed, "tp", axis=1, tiled=True),
        out_weight,
        preferred_element_type=jnp.float32,
    )
    return mixed.astype(jnp.bfloat16)


def solution(mesh):
    return jax.shard_map(
        on_device,
        mesh=mesh,
        in_specs=(
            P("seq", None),
            P("seq", "tp"),
            P("seq", "tp"),
            P("seq", "tp"),
            P("seq", "tp"),
            P("tp"),
            P("tp"),
            P(None, "tp"),
        ),
        out_specs=P("seq", "tp"),
        check_vma=False,
    )
```

profile of v0, /device:TPU:0, one launch (start us, length us, event | category | flops | bytes accessed | tf_op | source)
XLA Modules:
  0.0 327.7 jit_solution(9326917545958776825)
XLA Ops:
  6.5 0.7 all-gather.8.cloned.1.call-update
  7.3 0.7 all-gather.10.cloned.1.call-update
  8.1 0.7 all-gather.12.cloned.1.call-update
  8.8 0.7 neg.9
  9.4 33.2 %all_gather.21 = bf16[4096,4]{0,1:T(4,128)(2,1)S(1)} all-gather(bf16[512,4]{0,1:T(4,128)(2,1)} %param.12), channel_id=1, replica_groups=mesh['seq'=8,'tp'=4] {'seq'}, dimensions={0}, use_global_device_ids=true | all-gather | bytes 36864 | tf_op jit(solution)/shard_map/all_gather | solution.py:22
  42.7 4.5 %fusion.10 = f32[4,768]{1,0:T(4,128)S(1)} fusion(f32[4]{0:T(128)S(1)} %neg.9, bf16[4096,4]{0,1:T(4,128)(2,1)S(1)} %all_gather.21, bf16[768,4096]{1,0:T(8,128)(2,1)} %param.8), kind=kOutput, calls=%fused_computation.25 | convolution fusion | flops 25187328 | bytes 6336528 | tf_op jit(solution)/shard_map/dot_general | solution.py:16
  47.2 1.1 reduce-window.6
  49.1 36.1 %all-gather.8.cloned.1.call-done = bf16[4096,512]{1,0:T(8,128)(2,1)} async-done(((bf16[512,512]{1,0:T(8,128)(2,1)}), bf16[4096,512]{1,0:T(8,128)(2,1)}) %all-gather.8.cloned.1.call-update) | async-done | bytes 4194320 | tf_op jit(solution)/shard_map/all_gather | solution.py:20
  85.2 7.5 %convolution_convert_fusion.3 = bf16[768,512]{0,1:T(8,128)(2,1)S(1)} fusion(bf16[768,4096]{1,0:T(8,128)(2,1)} %param.8, bf16[4096,512]{1,0:T(8,128)(2,1)} %all-gather.8.cloned.1.call-done), kind=kOutput, calls=%fused_computation.17 | convolution fusion | flops 3221618688 | bytes 11272192 | tf_op jit(solution)/shard_map/dot_general | solution.py:16
  92.7 66.0 %all-gather.10.cloned.1.call-done = bf16[4096,512]{1,0:T(8,128)(2,1)} async-done(((bf16[512,512]{1,0:T(8,128)(2,1)}), bf16[4096,512]{1,0:T(8,128)(2,1)}) %all-gather.10.cloned.1.call-update) | async-done | bytes 4194320 | tf_op jit(solution)/shard_map/all_gather | solution.py:21
  158.7 7.5 %convolution_convert_fusion.2 = bf16[768,512]{0,1:T(8,128)(2,1)S(1)} fusion(bf16[768,4096]{1,0:T(8,128)(2,1)} %param.8, bf16[4096,512]{1,0:T(8,128)(2,1)} %all-gather.10.cloned.1.call-done), kind=kOutput, calls=%fused_computation.16 | convolution fusion | flops 3221618688 | bytes 11272192 | tf_op jit(solution)/shard_map/dot_general | solution.py:16
  166.2 0.9 copy-done.2
  167.0 1.1 fusion.6
  168.2 18.8 %all-gather.1 = f32[8,1,4]{2,1,0:T(1,128)S(1)} all-gather(f32[1,1,4]{2,1,0:T(1,128)S(1)} %bitcast.45), channel_id=1, replica_groups=mesh['seq'=8,'tp'=4] {'seq'}, dimensions={0}, use_global_device_ids=true | all-gather | bytes 144 | tf_op jit(solution)/shard_map/all_gather | solution.py:37
  187.7 1.0 iota_compare_fusion
  188.7 43.6 %all-gather.12.cloned.1.call-done = bf16[4096,512]{1,0:T(8,128)(2,1)} async-done(((bf16[512,512]{1,0:T(8,128)(2,1)}), bf16[4096,512]{1,0:T(8,128)(2,1)}) %all-gather.12.cloned.1.call-update) | async-done | bytes 4194320 | tf_op jit(solution)/shard_map/all_gather | solution.py:18
  232.2 7.5 %convolution_convert_fusion.1 = bf16[768,512]{0,1:T(8,128)(2,1)S(1)} fusion(bf16[768,4096]{1,0:T(8,128)(2,1)} %param.8, bf16[4096,512]{1,0:T(8,128)(2,1)} %all-gather.12.cloned.1.call-done), kind=kOutput, calls=%fused_computation.15 | convolution fusion | flops 3221618688 | bytes 11272192 | tf_op jit(solution)/shard_map/dot_general | solution.py:16
  240.1 5.7 %fusion = f32[4,128,768]{2,1,0:T(8,128)S(1)} fusion(bf16[768,4,128]{0,2,1:T(8,128)(2,1)} %bitcast.49, f32[4,768]{1,0:T(4,128)S(1)} %get-tuple-element.6, pred[768,768]{1,0:T(8,128)(4,1)} %iota_compare_fusion, bf16[768,4,128]{0,2,1:T(8,128)(2,1)S(1)} %bitcast.41, bf16[768,4,128]{0,2,1:T(8,128)(2,1)} %bitcast.47), kind=kOutput, calls=%fused_computation.1 | convolution fusion | flops 1219756032 | bytes 4534272 | tf_op jit(solution)/shard_map/hts,shv->thv/dot_general | solution.py:64
  245.8 36.0 %all-gather.16.cloned.1.call-done = f32[32,128,128]{2,1,0:T(8,128)} async-done(((f32[4,128,128]{2,1,0:T(8,128)}), f32[32,128,128]{2,1,0:T(8,128)}) %all-gather.16.cloned.1.call-update) | async-done | bytes 2097168 | tf_op jit(solution)/shard_map/all_gather | solution.py:41
  281.9 1.8 multiply_reduce_fusion
  283.7 1.3 fusion.5
  285.2 1.0 fusion.4
  286.2 27.2 %all-gather.14.cloned.1.call-done = bf16[768,2048]{0,1:T(8,128)(2,1)} async-done(((bf16[768,512]{0,1:T(8,128)(2,1)}), bf16[768,2048]{0,1:T(8,128)(2,1)}) %all-gather.14.cloned.1.call-update) | async-done | bytes 3145744 | tf_op jit(solution)/shard_map/all_gather | solution.py:74
  313.4 7.8 %convolution_convert_fusion = bf16[768,1024]{1,0:T(8,128)(2,1)} fusion(bf16[768,2048]{0,1:T(8,128)(2,1)} %all-gather.14.cloned.1.call-done, bf16[2048,1024]{1,0:T(8,128)(2,1)} %param.15), kind=kOutput, calls=%fused_computation.6 | convolution fusion | flops 3222011904 | bytes 8912896 | tf_op jit(solution)/shard_map/dot_general | solution.py:73
  (28 shorter events, 2.0 us)
Async XLA Ops:
  6.5 78.7 %all-gather.8.cloned.1.call-start = ((), (), s32[]{:S(2)}) async-start(), calls=%async_computation | async-start | bytes 4718592 | tf_op jit(solution)/shard_map/all_gather | solution.py:20
  7.3 151.4 %all-gather.10.cloned.1.call-start = ((), (), s32[]{:S(2)}) async-start(), calls=%async_computation.1 | async-start | bytes 4718592 | tf_op jit(solution)/shard_map/all_gather | solution.py:21
  8.0 224.2 %all-gather.12.cloned.1.call-start = ((), (), s32[]{:S(2)}) async-start(), calls=%async_computation.2 | async-start | bytes 4718592 | tf_op jit(solution)/shard_map/all_gather | solution.py:18
  8.7 273.1 %all-gather.16.cloned.1.call-start = ((), (), s32[]{:S(2)}) async-start(), calls=%async_computation.4 | async-start | bytes 2359296 | tf_op jit(solution)/shard_map/all_gather | solution.py:41
  92.7 73.5 %copy-start.1 = (bf16[768,512]{0,1:T(8,128)(2,1)}, bf16[768,512]{0,1:T(8,128)(2,1)S(1)}, u32[]{:S(2)}) copy-start(bf16[768,512]{0,1:T(8,128)(2,1)S(1)} %convolution_convert_fusion.3) | copy-start | bytes 2359300
  166.2 0.9 copy-start.2
  168.2 145.2 %all-gather.14.cloned.1.call-start = ((), (), s32[]{:S(2)}) async-start(), calls=%async_computation.3 | async-start | bytes 3932160 | tf_op jit(solution)/shard_map/all_gather | solution.py:74
  283.7 1.5 copy-start
Sparse Core Ops, SparseCore 0:
  9.5 75.6 all-gather.7
  87.3 71.3 all-gather.9
  160.8 71.3 all-gather.11
  234.2 47.5 all-gather.15
  286.3 27.0 all-gather.13
where the time goes:
time: 328 us
  waiting for transfers between devices  211 us (64%)
  blocking collectives  52.1 us (16%)
  matrix products  42.8 us (13%)
  between operations  13.3 us (4%)
  other arithmetic  6.38 us (2%)
    all_gather x1, waiting for transfers between devices, on_device(): lax.all_gather(value_weight, 'seq', axis=0, tiled=True)  66 us
    all_gather x1, waiting for transfers between devices, on_device(): lax.all_gather(query_weight, 'seq', axis=0, tiled=True)  43.6 us
    all_gather x1, waiting for transfers between devices, on_device(): lax.all_gather(key_weight, 'seq', axis=0, tiled=True)  36.1 us
    all_gather x1, waiting for transfers between devices, on_device(): piece = lax.all_gather(shard_local_state[None], 'seq', axis=0, tiled=True)  36 us
    all_gather x1, blocking collectives, on_device(): lax.all_gather(gate_weight, 'seq', axis=0, tiled=True)  33.2 us
    all_gather x1, waiting for transfers between devices, on_device(): lax.all_gather(normed, 'tp', axis=1, tiled=True)  27.2 us
    dot_general x4, matrix products, contract(): return jnp.dot(tokens, piece, preferred_element_type=jnp.float32)  26.9 us
    all_gather x1, blocking collectives, on_device(): all_totals = lax.all_gather(block_total[None, :], 'seq', axis=0, tiled=True)  18.8 us
  transfers between devices with their start and end apart: 5, of which 5 were waited for; matrix products, arithmetic and copies ran while one was open for 12% of the time, Pallas kernels for 0%

commit v1 on v0

v1 whole, which is shorter than its diff:
```python
import functools

import jax
import jax.numpy as jnp
from jax import lax
from jax.experimental import pallas as pl
from jax.experimental.pallas import tpu as pltpu
from jax.sharding import PartitionSpec as P


BF = jnp.bfloat16
F32 = jnp.float32


def cost(flops, nbytes, trans=0):
    return pl.CostEstimate(flops=int(flops), bytes_accessed=int(nbytes), transcendentals=int(trans))


def params(mib):
    return pltpu.CompilerParams(vmem_limit_bytes=mib * 2**20)


VMEM = pl.BlockSpec(memory_space=pltpu.VMEM)


def call(kernel, out_shape, args, estimate, mib=14):
    return pl.pallas_call(
        kernel,
        out_shape=out_shape,
        in_specs=[VMEM] * len(args),
        compiler_params=params(mib),
        cost_estimate=estimate,
    )(*args)


def flag(flags_ref, row, shape):
    return jnp.broadcast_to(flags_ref[row : row + 1, 0:1], shape) > 0.5


def turn_kernel(where, tok_ref, *refs, planes, rows, other, tile):
    out_refs, sem = refs[:-1], refs[-1]
    plane = where[0] ^ other
    half = where[1]
    merged = rows % 128 != 0
    unit = 2 * rows if merged else rows
    copies = []
    for i in range(tok_ref.shape[1] // unit):
        if merged:
            block = lax.rem(plane + i, planes)
        else:
            block = lax.rem(plane + i // 2, planes) * 2 + (half if i % 2 == 0 else 1 - half)
        cols = pl.ds(pl.multiple_of(block * unit, unit), unit)
        first = pl.multiple_of(where[3] * tile, tile) if tile else 0
        for out_ref in out_refs:
            copies.append(
                pltpu.make_async_copy(
                    tok_ref.at[pl.ds(first, out_ref.shape[0]), cols],
                    out_ref.at[:, pl.ds(i * unit, unit)],
                    sem.at[len(copies)],
                )
            )
            copies[-1].start()
            first = first + out_ref.shape[0]
    for copy in copies:
        copy.wait()


def turn(where, tokens, planes, rows, tile, sizes, other, mib):
    width = tokens.shape[1]
    unit = 2 * rows if rows % 128 else rows
    return pl.pallas_call(
        functools.partial(turn_kernel, planes=planes, rows=rows, other=other, tile=tile),
        out_shape=[jax.ShapeDtypeStruct((size, width), BF) for size in sizes],
        in_specs=[
            pl.BlockSpec(memory_space=pltpu.SMEM),
            pl.BlockSpec(memory_space=pltpu.HBM),
        ],
        out_specs=[VMEM] * len(sizes),
        scratch_shapes=[pltpu.SemaphoreType.DMA((len(sizes) * width // unit,))],
        compiler_params=params(mib),
        cost_estimate=cost(1e6, 4 * sum(sizes) * width),
    )(where, tokens)


def pack_kernel(flags_ref, k_ref, v_ref, q_ref, *out_refs, groups, size, hp):
    refs = {"k": k_ref, "v": v_ref, "q": q_ref}
    odd = flag(flags_ref, 1, (k_ref.shape[0], size))
    for o, (head, names) in enumerate(groups):
        for j, n in enumerate(names):
            low = refs[n][:, head * size : (head + 1) * size]
            high = refs[n][:, (hp + head) * size : (hp + head + 1) * size]
            out_refs[2 * o][:, j * size : (j + 1) * size] = jnp.where(odd, high, low)
            out_refs[2 * o + 1][:, j * size : (j + 1) * size] = jnp.where(odd, low, high)


def decay_kernel(flags_ref, tok_ref, gate_ref, rate_ref, out_ref, *, hp):
    logit = lax.dot_general(
        gate_ref[...], tok_ref[...], (((1,), (1,)), ((), ())), preferred_element_type=F32
    )
    logit = logit[0 : rate_ref.shape[0], :]
    soft = jnp.maximum(logit, 0.0) + jnp.log1p(jnp.exp(-jnp.abs(logit)))
    run = -rate_ref[...] * soft
    lane = lax.broadcasted_iota(jnp.int32, run.shape, 1)
    step = 1
    while step < run.shape[1]:
        run = run + jnp.where(lane >= step, pltpu.roll(run, step, 1), 0.0)
        step *= 2
    odd = flag(flags_ref, 1, (hp, run.shape[1]))
    low, high = run[0:hp, :], run[hp : 2 * hp, :]
    out_ref[...] = jnp.zeros_like(out_ref)
    out_ref[0:hp, :] = jnp.where(odd, high, low)
    out_ref[hp : 2 * hp, :] = jnp.where(odd, low, high)


def project_kernel(flags_ref, *refs, parts, n_tp):
    tok_refs, block_refs, out_ref = refs[:parts], refs[parts:-1], refs[-1]
    rows = block_refs[0].shape[0]
    cols = out_ref.shape[1]
    tok_rows = out_ref.shape[0]
    tile = tok_rows // n_tp

    def product(pick):
        acc = None
        for i, block_ref in enumerate(block_refs):
            part = jnp.dot(
                pick(slice(i * rows, (i + 1) * rows)), block_ref[...], preferred_element_type=F32
            )
            acc = part if acc is None else acc + part
        return acc

    if parts == 1:
        big = 256 if tok_rows % 256 == 0 else tile
        for r in range(tok_rows // big):
            cut = slice(r * big, (r + 1) * big)
            out_ref[cut, :] = product(lambda at: tok_refs[0][cut, at]).astype(BF)
        return
    each = parts // n_tp
    got = []
    for r in range(0, n_tp, 2):
        acc = product(
            lambda at: jnp.concatenate([ref[:, at] for ref in tok_refs[r * each : (r + 2) * each]], axis=0)
        )
        got += [acc[:tile].astype(BF), acc[tile:].astype(BF)]
    bit, row = 1, 2
    while bit < n_tp:
        swap = flag(flags_ref, row, (tile, cols))
        got = [jnp.where(swap, got[i ^ bit], got[i]) for i in range(n_tp)]
        bit, row = 2 * bit, row + 1
    for i in range(n_tp):
        out_ref[i * tile : (i + 1) * tile, :] = got[i]


def project(flags, first, toks, blocks, n_tp):
    tok_rows = sum(t.shape[0] for t in toks)
    width, cols = toks[0].shape[1], blocks[0].shape[1]
    if blocks[0].shape[0] % 128:
        blocks = [
            jnp.concatenate([jnp.where(first, a, b), jnp.where(first, b, a)], axis=0)
            for a, b in zip(blocks[0::2], blocks[1::2])
        ]
    return call(
        functools.partial(project_kernel, parts=len(toks), n_tp=n_tp),
        jax.ShapeDtypeStruct((tok_rows, cols), BF),
        (flags, *toks, *blocks),
        cost(2 * tok_rows * width * max(cols, 256), 2 * tok_rows * width),
        16,
    )


def spread(row, size):
    return jnp.broadcast_to(row, (size, row.shape[1])).T


def state_kernel(own_ref, far_ref, win_ref, winp_ref, out_ref, *, head, hp, size):
    for b, (kv_ref, row) in enumerate(
        ((own_ref, win_ref[head : head + 1, :]), (far_ref, winp_ref[hp + head : hp + head + 1, :]))
    ):
        total = row[:, row.shape[1] - 1 :]
        key = kv_ref[:, 0:size].astype(F32)
        scaled = (spread(jnp.exp(total - row), size) * key).astype(BF)
        out_ref[b, 0:size, :] = lax.dot_general(
            scaled, kv_ref[:, size : 2 * size], (((0,), (0,)), ((), ())), preferred_element_type=F32
        )
        out_ref[b, size:, :] = jnp.broadcast_to(total, (8, size))


def in_order(flags_ref, near_ref, far_ref, size):
    second = flag(flags_ref, 0, near_ref.shape[1:])
    odd = flag(flags_ref, 1, near_ref.shape[1:])
    low, high = [], []
    for ref in (near_ref, far_ref):
        own, partner = ref[0], ref[1]
        low.append(jnp.where(odd, partner, own))
        high.append(jnp.where(odd, own, partner))
    both = []
    for near, far in (low, high):
        both += [jnp.where(second, far, near), jnp.where(second, near, far)]
    return [x[0:size, :] for x in both], [jnp.exp(x[size : size + 1, :]) for x in both]


def quad_kernel(flags_ref, near_ref, far_ref, *refs, size):
    (s0, s1, s2, s3), (d0, d1, d2, d3) = in_order(flags_ref, near_ref, far_ref, size)
    state = s0
    if len(refs) == 2:
        state = d0 * refs[0][...] + s0
    refs[-1][...] = d3 * (d2 * (d1 * state + s1) + s2) + s3


def mix_kernel(flags_ref, *refs, which, head, hp, size, tile, starts):
    kvq, refs = refs[: 2 * len(which)], refs[2 * len(which) :]
    windows, refs = refs[: len(which)], refs[len(which) :]
    near_ref, far_ref, gain_ref = refs[:3]
    out_refs = refs[-len(which) :]
    (s0, s1, s2, _), (d0, d1, d2, _) = in_order(flags_ref, near_ref, far_ref, size)
    p0 = refs[3][...] if starts else jnp.zeros_like(s0)
    p1 = d0 * p0 + s0
    p2 = d1 * p1 + s1
    p3 = d2 * p2 + s2
    second, odd = flag(flags_ref, 0, (size, size)), flag(flags_ref, 1, (size, size))
    low = jnp.where(second, p1, p0)
    high = jnp.where(second, p3, p2)
    gain = jnp.where(
        flag(flags_ref, 1, (1, size)),
        gain_ref[hp + head : hp + head + 1, :],
        gain_ref[head : head + 1, :],
    )
    for n, b in enumerate(which):
        kv_ref, q_ref = kvq[2 * n], kvq[2 * n + 1]
        q_at = q_ref.shape[1] - size
        state = (jnp.where(odd, low, high) if b else jnp.where(odd, high, low)).astype(BF)
        at = b * hp + head
        row = windows[n][at : at + 1, :]
        wide = spread(row, size)
        tok_rows = kv_ref.shape[0]
        for i in range(tok_rows // tile):
            lo, hi = i * tile, (i + 1) * tile
            query = q_ref[lo:hi, q_at:]
            wide_i = wide[lo:hi, :]
            scores = lax.dot_general(
                query, kv_ref[0:hi, 0:size], (((1,), (1,)), ((), ())), preferred_element_type=F32
            )
            gap = wide_i[:, 0:1] - row[:, 0:hi]
            row_index = lo + lax.broadcasted_iota(jnp.int32, (tile, hi), 0)
            col_index = lax.broadcasted_iota(jnp.int32, (tile, hi), 1)
            causal = col_index <= row_index
            attn = jnp.where(causal, scores * jnp.exp(jnp.where(causal, gap, 0.0)), 0.0).astype(BF)
            local = jnp.dot(attn, kv_ref[0:hi, size : 2 * size], preferred_element_type=F32)
            scaled = (jnp.exp(wide_i) * query.astype(F32)).astype(BF)
            carried = jnp.dot(scaled, state, preferred_element_type=F32)
            head_out = carried + local
            mean_square = jnp.mean(head_out * head_out, axis=-1, keepdims=True)
            normed = head_out * lax.rsqrt(mean_square + 1e-05) * gain
            out_refs[n][lo:hi, :] = normed.astype(BF)


def join_kernel(a_ref, b_ref, out_ref):
    out_ref[:, : a_ref.shape[1]] = a_ref[...]
    out_ref[:, a_ref.shape[1] :] = b_ref[...]


def out_kernel(flags_ref, weight_ref, *refs, n_tp, heads, hp, head, flags, size, acc):
    out_ref = refs[-1]
    normed = refs[: len(refs) - 1 - acc]
    cols = out_ref.shape[1]
    odd = flag(flags_ref, 1, (size, cols))
    pieces = []
    for other in flags:
        rows = []
        for t in range(n_tp):
            low = weight_ref[(t * heads + head) * size : (t * heads + head + 1) * size, :]
            at = t * heads + hp + head
            high = weight_ref[at * size : (at + 1) * size, :]
            rows.append(jnp.where(odd, low, high) if other else jnp.where(odd, high, low))
        bit, row = 1, 2
        while bit < n_tp:
            swap = flag(flags_ref, row, (size, cols))
            rows = [jnp.where(swap, rows[i ^ bit], rows[i]) for i in range(n_tp)]
            bit, row = 2 * bit, row + 1
        pieces += rows
    total = None
    wide = normed[0].shape[1] // size
    tok_rows = out_ref.shape[0]
    tile = 256 if tok_rows % 256 == 0 else tok_rows
    right = jnp.concatenate(pieces, axis=0)
    for r in range(tok_rows // tile):
        cut = slice(r * tile, (r + 1) * tile)
        left = [ref[cut, f * size : (f + 1) * size] for f in range(wide) for ref in normed]
        total = jnp.dot(jnp.concatenate(left, axis=1), right, preferred_element_type=F32)
        if acc:
            total = total + refs[-2][cut, :]
        out_ref[cut, :] = total.astype(out_ref.dtype)


def solution(mesh):
    n_seq, n_tp = mesh.shape["seq"], mesh.shape["tp"]
    planes = n_seq // 2
    hops = n_seq // 4 - 1
    bits = [1 << b for b in reversed(range((n_tp - 1).bit_length()))]
    steps = sorted(range(1, planes), key=lambda k: (k % 2 == 0, min(k, planes - k), k))

    def from_plane(step):
        return [(2 * ((z + step) % planes) + y, 2 * z + y) for z in range(planes) for y in (0, 1)]

    half_swap = [(s, s ^ 1) for s in range(n_seq)]
    pair_swap = [(s, s ^ 2) for s in range(n_seq)]
    quad_up = [(s, s + 4) for s in range(n_seq - 4)]

    def over_tp(own):
        got = {0: own}
        for bit in bits:
            swap = [(t, t ^ bit) for t in range(n_tp)]
            got.update({i ^ bit: lax.ppermute(v, "tp", swap) for i, v in list(got.items())})
        return [got[i] for i in range(n_tp)]

    def body(
        tokens, query_weight, key_weight, value_weight, gate_weight, decay_rate, norm_gain, out_weight
    ):
        tok_rows, width = tokens.shape
        heads = decay_rate.shape[0]
        hp = heads // 2
        size = query_weight.shape[1] // heads
        tp = lax.axis_index("tp")
        rank = lax.axis_index("seq")
        half = rank % 2
        plane = rank // 2
        par = plane % 2
        where = jnp.stack([plane, half, par, tp]).astype(jnp.int32)
        tp_bits = [(tp >> b) & 1 for b in range((n_tp - 1).bit_length())]
        flags = jnp.stack([half, par, *tp_bits] + [par] * (6 - len(tp_bits))).astype(F32)
        flags = jnp.broadcast_to(flags[:, None], (8, 128))
        groups = [(h, "kvq") for h in range(hp - 1)] + [(hp - 1, "kv"), (hp - 1, "q")]
        rows = key_weight.shape[0]

        tile = tok_rows // n_tp
        last = tile // 3 if tile % 48 == 0 else tile // 2
        sizes = (tile - last, last)
        chunks = len(sizes)
        mine = turn(where, tokens, planes, rows, tile, sizes, 1, 61)
        pieces = [None] * (n_tp * chunks)
        for c in range(chunks):
            got = over_tp(lax.ppermute(mine[c], "seq", pair_swap))
            for i in range(n_tp):
                pieces[i * chunks + c] = got[i]
        (own_tokens,) = turn(where, tokens, planes, rows, 0, (tok_rows,), 0, 52)

        packed = call(
            functools.partial(pack_kernel, groups=groups, size=size, hp=hp),
            [
                jax.ShapeDtypeStruct((rows, len(names) * size), BF)
                for _, names in groups
                for _ in (0, 1)
            ],
            (flags, key_weight, value_weight, query_weight),
            cost(1e6, key_weight.size * 12),
        )

        def gather(g):
            keep, give = packed[2 * g], packed[2 * g + 1]
            got = {0: keep}
            for k in steps:
                got[k] = lax.ppermute(give if k % 2 else keep, "seq", from_plane(k))
            blocks = []
            for k in range(planes):
                blocks += [got[k], lax.ppermute(got[k], "seq", half_swap)]
            return blocks

        gathered = [gather(g) for g in range(len(groups))]

        gate = gate_weight.T
        gate_z = {k: lax.ppermute(gate, "seq", from_plane(k)) for k in steps}
        gate_z = jnp.stack([gate] + [gate_z[k] for k in range(1, planes)])
        gate_zy = lax.ppermute(gate_z, "seq", half_swap)
        if rows % 128:
            gate_z, gate_zy = (
                jnp.where(half == 0, gate_z, gate_zy),
                jnp.where(half == 0, gate_zy, gate_z),
            )
        gate_all = jnp.concatenate([gate_z, gate_zy], axis=2)
        gate_all = gate_all.transpose(1, 0, 2).reshape(heads, width)
        rows8 = -(-heads // 8) * 8
        gate_all = jnp.pad(gate_all, ((0, 2 * rows8 - heads), (0, 0)))
        rate = jnp.pad(decay_rate[:, None], ((0, rows8 - heads), (0, 0)))
        within = call(
            functools.partial(decay_kernel, hp=hp),
            jax.ShapeDtypeStruct((rows8, tok_rows), F32),
            (flags, own_tokens, gate_all, rate),
            cost(64 * tok_rows * width, 2 * tok_rows * width),
        )
        within_far = lax.ppermute(within, "seq", pair_swap)
        gain = norm_gain.reshape(heads, size)

        own_proj, far_proj = [], []
        for blocks in gathered:
            far_proj.append(project(flags, half == 0, pieces, blocks, n_tp))
            own_proj.append(project(flags, half == 0, [own_tokens], blocks, n_tp))
        proj = list(zip(own_proj, far_proj))
        acc = []

        def out(normed, head, other, last):
            return call(
                functools.partial(
                    out_kernel,
                    n_tp=n_tp,
                    heads=heads,
                    hp=hp,
                    head=head,
                    flags=other,
                    size=size,
                    acc=len(acc),
                ),
                jax.ShapeDtypeStruct((tok_rows, out_weight.shape[1]), BF if last else F32),
                (flags, out_weight, *normed, *acc),
                cost(
                    2 * tok_rows * size * n_tp * len(other) * out_weight.shape[1],
                    2 * out_weight.size,
                ),
                20,
            )

        for head in range(hp):
            kv = proj[head]
            q = proj[-1] if head == hp - 1 else kv
            local = call(
                functools.partial(state_kernel, head=head, hp=hp, size=size),
                jax.ShapeDtypeStruct((2, size + 8, size), F32),
                (kv[0], kv[1], within, within_far),
                cost(4 * tok_rows * size * size, 16 * tok_rows * size),
            )
            far = lax.ppermute(local, "seq", half_swap)
            start = []
            for _ in range(hops):
                quad = call(
                    functools.partial(quad_kernel, size=size),
                    jax.ShapeDtypeStruct((size, size), F32),
                    (flags, local, far, *start),
                    cost(1e6, 40 * size * size),
                )
                start = [lax.ppermute(quad, "seq", quad_up)]

            def mix(which):
                kvq = [a for b in which for a in (kv[b], q[b])]
                windows = [(within, within_far)[b] for b in which]
                shape = jax.ShapeDtypeStruct((tok_rows, size), BF)
                return call(
                    functools.partial(
                        mix_kernel,
                        which=which,
                        head=head,
                        hp=hp,
                        size=size,
                        tile=256 if tok_rows % 256 == 0 else tok_rows,
                        starts=len(start),
                    ),
                    [shape] * len(which),
                    (flags, *kvq, *windows, local, far, gain, *start),
                    cost(
                        4 * tok_rows * tok_rows * size * len(which),
                        12 * tok_rows * size,
                        tok_rows * tok_rows,
                    ),
                )

            if head < hp - 1:
                normed, normed_far = mix((0, 1))
                back = lax.ppermute(normed_far, "seq", pair_swap)
                both = call(
                    join_kernel,
                    jax.ShapeDtypeStruct((tok_rows, 2 * size), BF),
                    (normed, back),
                    cost(1e6, 8 * tok_rows * size),
                )
                both = over_tp(both)
                acc = [out(both, head, (0, 1), False)]
            else:
                (normed_far,) = mix((1,))
                back = lax.ppermute(normed_far, "seq", pair_swap)
                (normed,) = mix((0,))
                acc = [out(over_tp(normed), head, (0,), False)]
                return out(over_tp(back), head, (1,), True)

    return jax.shard_map(
        body,
        mesh=mesh,
        in_specs=(
            P("seq", None),
            P("seq", "tp"),
            P("seq", "tp"),
            P("seq", "tp"),
            P("seq", "tp"),
            P("tp"),
            P("tp"),
            P(None, "tp"),
        ),
        out_specs=P("seq", "tp"),
        check_vma=False,
    )
```

time: 328 us -> 217 us (0.66)
  waiting for transfers between devices: 211 us -> 99.6 us
  starting transfers between devices: 0.16 us -> 58.3 us
  blocking collectives: 52.1 us -> 0 us
  Pallas kernels: 0 us -> 44.6 us
  matrix products: 42.8 us -> 0 us
  between operations: 13.3 us -> 0.64 us
  local copies, waits for them, and re-layouts: 1.97 us -> 12.9 us
  other arithmetic: 6.38 us -> 0.7 us
    all_gather x5 -> x0, waiting for transfers between devices: 209 us -> none  [the longest x1 66 us: on_device(): lax.all_gather(value_weight, 'seq', axis=0, tiled=True)]
    ppermute x0 -> x49, waiting for transfers between devices: none -> 99.6 us  [the longest x9 32.8 us: gather(): got[k] = lax.ppermute(give if k % 2 else keep, 'seq', from_plane(k))]
    ppermute x0 -> x49, starting transfers between devices: none -> 58.3 us  [the longest x9 15.5 us: gather(): got[k] = lax.ppermute(give if k % 2 else keep, 'seq', from_plane(k))]
    all_gather x2 -> x0, blocking collectives: 52.1 us -> none  [the longest x1 33.2 us: on_device(): lax.all_gather(gate_weight, 'seq', axis=0, tiled=True)]
    pallas_call x0 -> x21, Pallas kernels: none -> 44.6 us  [the longest x19 34.9 us: call(): pl.pallas_call(kernel, out_shape=out_shape, in_specs=[VMEM] * len(args),...]
    dot_general x8 -> x0, matrix products: 42.8 us -> none  [the longest x4 26.9 us: contract(): return jnp.dot(tokens, piece, preferred_element_type=jnp.float32)]
    unnamed x6 -> x70, local copies, waits for them, and re-layouts: 0.87 us -> 10.7 us
  transfers between devices with their start and end apart: 5 -> 49, of which waited for: 5 -> 14; matrix products, arithmetic and copies ran while one was open for 12% -> 1% of each run, Pallas kernels for 0% -> 17%
where the time goes in v1:
time: 217 us
  waiting for transfers between devices  99.6 us (46%)
  starting transfers between devices  58.3 us (27%)
  Pallas kernels  44.6 us (21%)
  local copies, waits for them, and re-layouts  12.9 us (6%)
    pallas_call x19, Pallas kernels, call(): pl.pallas_call(kernel, out_shape=out_shape, in_specs=[VMEM] * len(args),...  34.9 us
    ppermute x9, waiting for transfers between devices, gather(): got[k] = lax.ppermute(give if k % 2 else keep, 'seq', from_plane(k))  32.8 us
    ppermute x2, waiting for transfers between devices, body(): got = over_tp(lax.ppermute(mine[c], 'seq', pair_swap))  23.4 us
    ppermute x2, waiting for transfers between devices, body(): far = lax.ppermute(local, 'seq', half_swap)  15.9 us
    ppermute x9, starting transfers between devices, gather(): got[k] = lax.ppermute(give if k % 2 else keep, 'seq', from_plane(k))  15.5 us
    ppermute x12, starting transfers between devices, gather(): blocks += [got[k], lax.ppermute(got[k], 'seq', half_swap)]  14.8 us
    unnamed x70, local copies, waits for them, and re-layouts  10.7 us
    pallas_call x2, Pallas kernels, turn(): pl.pallas_call(functools.partial(turn_kernel, planes=planes, rows=rows, o...  9.67 us
  transfers between devices with their start and end apart: 49, of which 14 were waited for; matrix products, arithmetic and copies ran while one was open for 1% of the time, Pallas kernels for 17%

profile of v1, /device:TPU:0, one launch (start us, length us, event | category | flops | bytes accessed | tf_op | source)
XLA Modules:
  0.0 216.8 jit_solution(2654421931923569232)
XLA Ops:
  0.7 3.5 %shard_map.82 = (bf16[128,4096]{1,0:T(8,128)(2,1)}, bf16[64,4096]{1,0:T(8,128)(2,1)}) custom-call(s32[4]{0:T(128)} %pad_add_fusion.where, bf16[768,4096]{1,0:T(8,128)(2,1)} %tok_ref.3), custom_call_target="tpu_custom_call" | custom-call | flops 1000000 | bytes 3145728 | tf_op jit(solution)/shard_map/pallas_call | solution.py:71
  4.2 3.2 %collective-permute-start = (bf16[128,4096]{1,0:T(8,128)(2,1)}, bf16[128,4096]{1,0:T(8,128)(2,1)S(1)}, u32[]{:S(2)}, u32[]{:S(2)}) collective-permute-start(bf16[128,4096]{1,0:T(8,128)(2,1)} %get-tuple-element.15), channel_id=1, source_target_pairs={{0,8},{4,12},{8,0},{12,4},{16,24},{20,28},{24,16},{28,20},{1,9},{5... | collective-permute-start | bytes 3145736 | tf_op jit(solution)/shard_map/ppermute | solution.py:341
  7.4 23.4 %collective-permute-done.refs_0_ = bf16[128,4096]{1,0:T(8,128)(2,1)S(1)} collective-permute-done((bf16[128,4096]{1,0:T(8,128)(2,1)}, bf16[128,4096]{1,0:T(8,128)(2,1)S(1)}, u32[]{:S(2)}, u32[]{:S(2)}) %collective-permute-start) | collective-permute-done | bytes 1048608 | tf_op jit(solution)/shard_map/ppermute | solution.py:341
  37.5 2.6 %collective-permute-start.23 = (bf16[4,512]{1,0:T(4,128)(2,1)S(1)}, bf16[4,512]{1,0:T(4,128)(2,1)S(1)}, u32[]{:S(2)}, u32[]{:S(2)}) collective-permute-start(bf16[4,512]{1,0:T(4,128)(2,1)S(1)} %bitcast.21), channel_id=1, source_target_pairs={{16,0},{20,4},{24,8},{28,12},{0,16},{4,20},{8,24},{12,28},{17,1},{... | collective-permute-start | bytes 12296 | tf_op jit(solution)/shard_map/ppermute | solution.py:370
  42.2 7.1 %collective-permute-done.23 = bf16[4,512]{1,0:T(4,128)(2,1)S(1)} collective-permute-done((bf16[4,512]{1,0:T(4,128)(2,1)S(1)}, bf16[4,512]{1,0:T(4,128)(2,1)S(1)}, u32[]{:S(2)}, u32[]{:S(2)}) %collective-permute-start.23) | collective-permute-done | bytes 4128 | tf_op jit(solution)/shard_map/ppermute | solution.py:370
  49.3 3.8 %collective-permute-start.9 = (bf16[512,256]{1,0:T(8,128)(2,1)S(1)}, bf16[512,256]{1,0:T(8,128)(2,1)S(1)}, u32[]{:S(2)}, u32[]{:S(2)}) collective-permute-start(bf16[512,256]{1,0:T(8,128)(2,1)S(1)} %get-tuple-element.18), channel_id=1, source_target_pairs={{8,0},{12,4},{16,8},{20,12},{24,16},{28,20},{0,24},{4,28},{9,1},{1... | collective-permute-start | bytes 786440 | tf_op jit(solution)/shard_map/ppermute | solution.py:361
  57.8 6.6 %collective-permute-done.9.refs_10_.refs_3_ = bf16[512,256]{1,0:T(8,128)(2,1)S(1)} collective-permute-done((bf16[512,256]{1,0:T(8,128)(2,1)S(1)}, bf16[512,256]{1,0:T(8,128)(2,1)S(1)}, u32[]{:S(2)}, u32[]{:S(2)}) %collective-permute-start.9) | collective-permute-done | bytes 262176 | tf_op jit(solution)/shard_map/ppermute | solution.py:361
  64.4 4.8 %collective-permute-start.39 = (bf16[512,384]{1,0:T(8,128)(2,1)S(1)}, bf16[512,384]{1,0:T(8,128)(2,1)}, u32[]{:S(2)}, u32[]{:S(2)}) collective-permute-start(bf16[512,384]{1,0:T(8,128)(2,1)S(1)} %get-tuple-element.21.refs_1_.refs_8_), channel_id=1, source_target_pairs={{16,0},{20,4},{24,8},{28,12},{0,16},{4,20},{8,24},{12,28},{17,1},{... | collective-permute-start | bytes 1179656 | tf_op jit(solution)/shard_map/ppermute | solution.py:361
  70.8 16.4 %collective-permute-done.37.refs_3_.refs_10_ = bf16[512,384]{1,0:T(8,128)(2,1)S(1)} collective-permute-done((bf16[512,384]{1,0:T(8,128)(2,1)S(1)}, bf16[512,384]{1,0:T(8,128)(2,1)S(1)}, u32[]{:S(2)}, u32[]{:S(2)}) %collective-permute-start.37) | collective-permute-done | bytes 393248 | tf_op jit(solution)/shard_map/ppermute | solution.py:361
  92.6 3.3 %collective-permute-done.42.refs_8_.refs_15_ = bf16[512,384]{1,0:T(8,128)(2,1)S(1)} collective-permute-done((bf16[512,384]{1,0:T(8,128)(2,1)S(1)}, bf16[512,384]{1,0:T(8,128)(2,1)S(1)}, u32[]{:S(2)}, u32[]{:S(2)}) %collective-permute-start.42) | collective-permute-done | bytes 393248 | tf_op jit(solution)/shard_map/ppermute | solution.py:364
  99.1 5.2 %collective-permute-done.38.refs_4_.refs_11_ = bf16[512,384]{1,0:T(8,128)(2,1)S(1)} collective-permute-done((bf16[512,384]{1,0:T(8,128)(2,1)S(1)}, bf16[512,384]{1,0:T(8,128)(2,1)S(1)}, u32[]{:S(2)}, u32[]{:S(2)}) %collective-permute-start.38) | collective-permute-done | bytes 393248 | tf_op jit(solution)/shard_map/ppermute | solution.py:364
  107.7 6.1 %shard_map.86.tok_ref.refs_0_ = bf16[768,4096]{1,0:T(8,128)(2,1)} custom-call(s32[4]{0:T(128)S(1)} %copy-done.25, bf16[768,4096]{1,0:T(8,128)(2,1)} %tok_ref.3), custom_call_target="tpu_custom_call" | custom-call | flops 1000000 | bytes 12582912 | tf_op jit(solution)/shard_map/pallas_call | solution.py:71
  114.0 2.8 %copy-done = bf16[768,4096]{1,0:T(8,128)(2,1)S(1)} copy-done((bf16[768,4096]{1,0:T(8,128)(2,1)S(1)}, bf16[768,4096]{1,0:T(8,128)(2,1)}, u32[]{:S(2)}) %copy-start) | copy-done | bytes 6291480
  119.6 4.7 %shard_map.94.own_ref.refs_0_.refs_1_ = bf16[768,384]{1,0:T(8,128)(2,1)S(1)} custom-call(f32[8,128]{1,0:T(8,128)S(1)} %broadcast_in_dim.4.flags_ref, bf16[768,4096]{1,0:T(8,128)(2,1)S(1)} %copy-done.1, bf16[512,384]{1,0:T(8,128)(2,1)S(1)} %get-tuple-element.21.refs_1_.refs_8_, bf16[512,384]{1,0:T(8,128)(2,1)S(1)} %copy-done.8, ...), custom_call_target="tpu_custom_call" | custom-call | flops 2415919104 | bytes 6291456 | tf_op jit(solution)/shard_map/pallas_call | solution.py:27
  124.3 3.4 %collective-permute-done.11.refs_12_.refs_5_ = bf16[512,256]{1,0:T(8,128)(2,1)S(1)} collective-permute-done((bf16[512,256]{1,0:T(8,128)(2,1)S(1)}, bf16[512,256]{1,0:T(8,128)(2,1)S(1)}, u32[]{:S(2)}, u32[]{:S(2)}) %collective-permute-start.11) | collective-permute-done | bytes 262176 | tf_op jit(solution)/shard_map/ppermute | solution.py:361
  132.4 5.5 %shard_map.95.far_ref.refs_2_.refs_3_ = bf16[768,384]{1,0:T(8,128)(2,1)S(1)} custom-call(f32[8,128]{1,0:T(8,128)S(1)} %broadcast_in_dim.4.flags_ref, bf16[128,4096]{1,0:T(8,128)(2,1)S(1)} %collective-permute-done.refs_0_, bf16[64,4096]{1,0:T(8,128)(2,1)} %collective-permute-done.1.refs_1_, bf16[128,4096]{1,0:T(8,128)(2,1)S(1)} %collective-permute-done.2.refs_2_, ...), custom_call_target="tpu_custom_call" | custom-call | flops 2415919104 | bytes 6291456 | tf_op jit(solution)/shard_map/pallas_call | solution.py:27
  140.6 15.9 %collective-permute-done.43.far_ref.refs_7_ = f32[2,136,128]{2,1,0:T(8,128)S(1)} collective-permute-done((f32[2,136,128]{2,1,0:T(8,128)S(1)}, f32[2,136,128]{2,1,0:T(8,128)S(1)}, u32[]{:S(2)}, u32[]{:S(2)}) %collective-permute-start.43) | collective-permute-done | bytes 139296 | tf_op jit(solution)/shard_map/ppermute | solution.py:429
  162.7 3.6 %shard_map.84.far_ref.refs_0_ = bf16[768,256]{1,0:T(8,128)(2,1)S(1)} custom-call(f32[8,128]{1,0:T(8,128)S(1)} %broadcast_in_dim.4.flags_ref, bf16[128,4096]{1,0:T(8,128)(2,1)S(1)} %collective-permute-done.refs_0_, bf16[64,4096]{1,0:T(8,128)(2,1)} %collective-permute-done.1.refs_1_, bf16[128,4096]{1,0:T(8,128)(2,1)S(1)} %collective-permute-done.2.refs_2_, ...), custom_call_target="tpu_custom_call" | custom-call | flops 1610612736 | bytes 6291456 | tf_op jit(solution)/shard_map/pallas_call | solution.py:27
  174.1 2.9 %collective-permute-done.20.refs_14_.refs_7_ = bf16[512,128]{1,0:T(8,128)(2,1)S(1)} collective-permute-done((bf16[512,128]{1,0:T(8,128)(2,1)S(1)}, bf16[512,128]{1,0:T(8,128)(2,1)S(1)}, u32[]{:S(2)}, u32[]{:S(2)}) %collective-permute-start.20) | collective-permute-done | bytes 131104 | tf_op jit(solution)/shard_map/ppermute | solution.py:361
  179.0 3.5 %collective-permute-done.18.refs_12_.refs_5_ = bf16[512,128]{1,0:T(8,128)(2,1)S(1)} collective-permute-done((bf16[512,128]{1,0:T(8,128)(2,1)S(1)}, bf16[512,128]{1,0:T(8,128)(2,1)S(1)}, u32[]{:S(2)}, u32[]{:S(2)}) %collective-permute-start.18) | collective-permute-done | bytes 131104 | tf_op jit(solution)/shard_map/ppermute | solution.py:361
  184.6 4.7 %collective-permute-start.28 = (f32[128,128]{1,0:T(8,128)S(1)}, f32[128,128]{1,0:T(8,128)S(1)}, u32[]{:S(2)}, u32[]{:S(2)}) collective-permute-start(f32[128,128]{1,0:T(8,128)S(1)} %shard_map.90), channel_id=1, source_target_pairs={{0,16},{4,20},{8,24},{12,28},{1,17},{5,21},{9,25},{13,29},{2,18},{... | collective-permute-start | bytes 196616 | tf_op jit(solution)/shard_map/ppermute | solution.py:438
  189.4 3.6 %shard_map.85.refs_1_ = bf16[768,128]{1,0:T(8,128)(2,1)S(1)} custom-call(f32[8,128]{1,0:T(8,128)S(1)} %broadcast_in_dim.4.flags_ref, bf16[128,4096]{1,0:T(8,128)(2,1)S(1)} %collective-permute-done.refs_0_, bf16[64,4096]{1,0:T(8,128)(2,1)} %collective-permute-done.1.refs_1_, bf16[128,4096]{1,0:T(8,128)(2,1)S(1)} %collective-permute-done.2.refs_2_, ...), custom_call_target="tpu_custom_call" | custom-call | flops 1610612736 | bytes 6291456 | tf_op jit(solution)/shard_map/pallas_call | solution.py:27
  201.5 5.7 %collective-permute-done.34.refs_2_ = bf16[768,128]{1,0:T(8,128)(2,1)S(1)} collective-permute-done((bf16[768,128]{1,0:T(8,128)(2,1)S(1)}, bf16[768,128]{1,0:T(8,128)(2,1)S(1)}, u32[]{:S(2)}, u32[]{:S(2)}) %collective-permute-start.34) | collective-permute-done | bytes 196640 | tf_op jit(solution)/shard_map/ppermute | solution.py:312
  207.2 3.2 %collective-permute-done.31.refs_2_ = bf16[768,128]{1,0:T(8,128)(2,1)S(1)} collective-permute-done((bf16[768,128]{1,0:T(8,128)(2,1)S(1)}, bf16[768,128]{1,0:T(8,128)(2,1)S(1)}, u32[]{:S(2)}, u32[]{:S(2)}) %collective-permute-start.31) | collective-permute-done | bytes 196640 | tf_op jit(solution)/shard_map/ppermute | solution.py:312
  (174 shorter events, 70.5 us)
Async XLA Ops:
  4.2 26.5 %collective-permute-start = (bf16[128,4096]{1,0:T(8,128)(2,1)}, bf16[128,4096]{1,0:T(8,128)(2,1)S(1)}, u32[]{:S(2)}, u32[]{:S(2)}) collective-permute-start(bf16[128,4096]{1,0:T(8,128)(2,1)} %get-tuple-element.15), channel_id=1, source_target_pairs={{0,8},{4,12},{8,0},{12,4},{16,24},{20,28},{24,16},{28,20},{1,9},{5... | collective-permute-start | bytes 3145736 | tf_op jit(solution)/shard_map/ppermute | solution.py:341
  30.7 59.4 %collective-permute-start.4 = (bf16[128,4096]{1,0:T(8,128)(2,1)S(1)}, bf16[128,4096]{1,0:T(8,128)(2,1)S(1)}, u32[]{:S(2)}, u32[]{:S(2)}) collective-permute-start(bf16[128,4096]{1,0:T(8,128)(2,1)S(1)} %collective-permute-done.refs_0_), channel_id=1, source_target_pairs={{0,2},{1,3},{2,0},{3,1},{4,6},{5,7},{6,4},{7,5},{8,10},{9,11},{10,... | collective-permute-start | bytes 3145736 | tf_op jit(solution)/shard_map/ppermute | solution.py:312
  36.0 21.7 %collective-permute-start.13 = (bf16[512,256]{1,0:T(8,128)(2,1)S(1)}, bf16[512,256]{1,0:T(8,128)(2,1)S(1)}, u32[]{:S(2)}, u32[]{:S(2)}) collective-permute-start(bf16[512,256]{1,0:T(8,128)(2,1)S(1)} %get-tuple-element.18), channel_id=1, source_target_pairs={{24,0},{28,4},{0,8},{4,12},{8,16},{12,20},{16,24},{20,28},{25,1},{... | collective-permute-start | bytes 786440 | tf_op jit(solution)/shard_map/ppermute | solution.py:361
  49.3 20.0 %collective-permute-start.41 = (bf16[512,384]{1,0:T(8,128)(2,1)S(1)}, bf16[512,384]{1,0:T(8,128)(2,1)S(1)}, u32[]{:S(2)}, u32[]{:S(2)}) collective-permute-start(bf16[512,384]{1,0:T(8,128)(2,1)S(1)} %get-tuple-element.22), channel_id=1, source_target_pairs={{24,0},{28,4},{0,8},{4,12},{8,16},{12,20},{16,24},{20,28},{25,1},{... | collective-permute-start | bytes 1179656 | tf_op jit(solution)/shard_map/ppermute | solution.py:361
  49.3 15.1 %collective-permute-start.9 = (bf16[512,256]{1,0:T(8,128)(2,1)S(1)}, bf16[512,256]{1,0:T(8,128)(2,1)S(1)}, u32[]{:S(2)}, u32[]{:S(2)}) collective-permute-start(bf16[512,256]{1,0:T(8,128)(2,1)S(1)} %get-tuple-element.18), channel_id=1, source_target_pairs={{8,0},{12,4},{16,8},{20,12},{24,16},{28,20},{0,24},{4,28},{9,1},{1... | collective-permute-start | bytes 786440 | tf_op jit(solution)/shard_map/ppermute | solution.py:361
  57.7 31.8 %collective-permute-start.1 = (bf16[64,4096]{1,0:T(8,128)(2,1)}, bf16[64,4096]{1,0:T(8,128)(2,1)}, u32[]{:S(2)}, u32[]{:S(2)}) collective-permute-start(bf16[64,4096]{1,0:T(8,128)(2,1)} %get-tuple-element.16), channel_id=1, source_target_pairs={{0,8},{4,12},{8,0},{12,4},{16,24},{20,28},{24,16},{28,20},{1,9},{5... | collective-permute-start | bytes 1572872 | tf_op jit(solution)/shard_map/ppermute | solution.py:341
  57.7 29.5 %collective-permute-start.37 = (bf16[512,384]{1,0:T(8,128)(2,1)S(1)}, bf16[512,384]{1,0:T(8,128)(2,1)S(1)}, u32[]{:S(2)}, u32[]{:S(2)}) collective-permute-start(bf16[512,384]{1,0:T(8,128)(2,1)S(1)} %get-tuple-element.22), channel_id=1, source_target_pairs={{8,0},{12,4},{16,8},{20,12},{24,16},{28,20},{0,24},{4,28},{9,1},{1... | collective-permute-start | bytes 1179656 | tf_op jit(solution)/shard_map/ppermute | solution.py:361
  64.4 25.6 %collective-permute-start.39 = (bf16[512,384]{1,0:T(8,128)(2,1)S(1)}, bf16[512,384]{1,0:T(8,128)(2,1)}, u32[]{:S(2)}, u32[]{:S(2)}) collective-permute-start(bf16[512,384]{1,0:T(8,128)(2,1)S(1)} %get-tuple-element.21.refs_1_.refs_8_), channel_id=1, source_target_pairs={{16,0},{20,4},{24,8},{28,12},{0,16},{4,20},{8,24},{12,28},{17,1},{... | collective-permute-start | bytes 1179656 | tf_op jit(solution)/shard_map/ppermute | solution.py:361
  69.2 21.3 %collective-permute-start.36 = (bf16[512,384]{1,0:T(8,128)(2,1)S(1)}, bf16[512,384]{1,0:T(8,128)(2,1)S(1)}, u32[]{:S(2)}, u32[]{:S(2)}) collective-permute-start(bf16[512,384]{1,0:T(8,128)(2,1)S(1)} %get-tuple-element.21.refs_1_.refs_8_), channel_id=1, source_target_pairs={{0,4},{4,0},{8,12},{12,8},{16,20},{20,16},{24,28},{28,24},{1,5},{5... | collective-permute-start | bytes 1179656 | tf_op jit(solution)/shard_map/ppermute | solution.py:364
  89.5 15.7 %collective-permute-start.5 = (bf16[64,4096]{1,0:T(8,128)(2,1)}, bf16[64,4096]{1,0:T(8,128)(2,1)}, u32[]{:S(2)}, u32[]{:S(2)}) collective-permute-start(bf16[64,4096]{1,0:T(8,128)(2,1)} %collective-permute-done.1.refs_1_), channel_id=1, source_target_pairs={{0,2},{1,3},{2,0},{3,1},{4,6},{5,7},{6,4},{7,5},{8,10},{9,11},{10,... | collective-permute-start | bytes 1572872 | tf_op jit(solution)/shard_map/ppermute | solution.py:312
  90.0 40.2 %collective-permute-start.2 = (bf16[128,4096]{1,0:T(8,128)(2,1)S(1)}, bf16[128,4096]{1,0:T(8,128)(2,1)S(1)}, u32[]{:S(2)}, u32[]{:S(2)}) collective-permute-start(bf16[128,4096]{1,0:T(8,128)(2,1)S(1)} %collective-permute-done.refs_0_), channel_id=1, source_target_pairs={{0,1},{1,0},{2,3},{3,2},{4,5},{5,4},{6,7},{7,6},{8,9},{9,8},{10,11... | collective-permute-start | bytes 3145736 | tf_op jit(solution)/shard_map/ppermute | solution.py:312
  90.1 42.2 %collective-permute-start.6 = (bf16[128,4096]{1,0:T(8,128)(2,1)S(1)}, bf16[128,4096]{1,0:T(8,128)(2,1)}, u32[]{:S(2)}, u32[]{:S(2)}) collective-permute-start(bf16[128,4096]{1,0:T(8,128)(2,1)S(1)} %collective-permute-done.4.refs_4_), channel_id=1, source_target_pairs={{0,1},{1,0},{2,3},{3,2},{4,5},{5,4},{6,7},{7,6},{8,9},{9,8},{10,11... | collective-permute-start | bytes 3145736 | tf_op jit(solution)/shard_map/ppermute | solution.py:312
  96.7 17.2 %collective-permute-start.40 = (bf16[512,384]{1,0:T(8,128)(2,1)}, bf16[512,384]{1,0:T(8,128)(2,1)}, u32[]{:S(2)}, u32[]{:S(2)}) collective-permute-start(bf16[512,384]{1,0:T(8,128)(2,1)} %collective-permute-done.39.refs_5_.refs_12_), channel_id=1, source_target_pairs={{0,4},{4,0},{8,12},{12,8},{16,20},{20,16},{24,28},{28,24},{1,5},{5... | collective-permute-start | bytes 1179656 | tf_op jit(solution)/shard_map/ppermute | solution.py:364
  105.1 25.0 %collective-permute-start.3 = (bf16[64,4096]{1,0:T(8,128)(2,1)}, bf16[64,4096]{1,0:T(8,128)(2,1)}, u32[]{:S(2)}, u32[]{:S(2)}) collective-permute-start(bf16[64,4096]{1,0:T(8,128)(2,1)} %collective-permute-done.1.refs_1_), channel_id=1, source_target_pairs={{0,1},{1,0},{2,3},{3,2},{4,5},{5,4},{6,7},{7,6},{8,9},{9,8},{10,11... | collective-permute-start | bytes 1572872 | tf_op jit(solution)/shard_map/ppermute | solution.py:312
  105.1 25.0 %collective-permute-start.7 = (bf16[64,4096]{1,0:T(8,128)(2,1)}, bf16[64,4096]{1,0:T(8,128)(2,1)}, u32[]{:S(2)}, u32[]{:S(2)}) collective-permute-start(bf16[64,4096]{1,0:T(8,128)(2,1)} %collective-permute-done.5.refs_5_), channel_id=1, source_target_pairs={{0,1},{1,0},{2,3},{3,2},{4,5},{5,4},{6,7},{7,6},{8,9},{9,8},{10,11... | collective-permute-start | bytes 1572872 | tf_op jit(solution)/shard_map/ppermute | solution.py:312
  127.7 30.5 %collective-permute-start.8 = (bf16[512,256]{1,0:T(8,128)(2,1)S(1)}, bf16[512,256]{1,0:T(8,128)(2,1)S(1)}, u32[]{:S(2)}, u32[]{:S(2)}) collective-permute-start(bf16[512,256]{1,0:T(8,128)(2,1)S(1)} %copy-done.14), channel_id=1, source_target_pairs={{0,4},{4,0},{8,12},{12,8},{16,20},{20,16},{24,28},{28,24},{1,5},{5... | collective-permute-start | bytes 786440 | tf_op jit(solution)/shard_map/ppermute | solution.py:364
  130.2 28.1 %collective-permute-start.14 = (bf16[512,256]{1,0:T(8,128)(2,1)S(1)}, bf16[512,256]{1,0:T(8,128)(2,1)S(1)}, u32[]{:S(2)}, u32[]{:S(2)}) collective-permute-start(bf16[512,256]{1,0:T(8,128)(2,1)S(1)} %copy-done.16), channel_id=1, source_target_pairs={{0,4},{4,0},{8,12},{12,8},{16,20},{20,16},{24,28},{28,24},{1,5},{5... | collective-permute-start | bytes 786440 | tf_op jit(solution)/shard_map/ppermute | solution.py:364
  130.3 28.0 %collective-permute-start.10 = (bf16[512,256]{1,0:T(8,128)(2,1)S(1)}, bf16[512,256]{1,0:T(8,128)(2,1)S(1)}, u32[]{:S(2)}, u32[]{:S(2)}) collective-permute-start(bf16[512,256]{1,0:T(8,128)(2,1)S(1)} %copy-done.18), channel_id=1, source_target_pairs={{0,4},{4,0},{8,12},{12,8},{16,20},{20,16},{24,28},{28,24},{1,5},{5... | collective-permute-start | bytes 786440 | tf_op jit(solution)/shard_map/ppermute | solution.py:364
  132.3 26.0 %collective-permute-start.12 = (bf16[512,256]{1,0:T(8,128)(2,1)S(1)}, bf16[512,256]{1,0:T(8,128)(2,1)S(1)}, u32[]{:S(2)}, u32[]{:S(2)}) collective-permute-start(bf16[512,256]{1,0:T(8,128)(2,1)S(1)} %collective-permute-done.11.refs_12_.refs_5_), channel_id=1, source_target_pairs={{0,4},{4,0},{8,12},{12,8},{16,20},{20,16},{24,28},{28,24},{1,5},{5... | collective-permute-start | bytes 786440 | tf_op jit(solution)/shard_map/ppermute | solution.py:364
  138.6 17.9 %collective-permute-start.43 = (f32[2,136,128]{2,1,0:T(8,128)S(1)}, f32[2,136,128]{2,1,0:T(8,128)S(1)}, u32[]{:S(2)}, u32[]{:S(2)}) collective-permute-start(f32[2,136,128]{2,1,0:T(8,128)S(1)} %shard_map.96.near_ref.refs_6_), channel_id=1, source_target_pairs={{0,4},{4,0},{8,12},{12,8},{16,20},{20,16},{24,28},{28,24},{1,5},{5... | collective-permute-start | bytes 417800 | tf_op jit(solution)/shard_map/ppermute | solution.py:429
  167.0 16.2 %collective-permute-start.27 = (f32[2,136,128]{2,1,0:T(8,128)S(1)}, f32[2,136,128]{2,1,0:T(8,128)S(1)}, u32[]{:S(2)}, u32[]{:S(2)}) collective-permute-start(f32[2,136,128]{2,1,0:T(8,128)S(1)} %shard_map.89.near_ref.refs_3_), channel_id=1, source_target_pairs={{0,4},{4,0},{8,12},{12,8},{16,20},{20,16},{24,28},{28,24},{1,5},{5... | collective-permute-start | bytes 417800 | tf_op jit(solution)/shard_map/ppermute | solution.py:429
  174.0 21.9 %collective-permute-start.47 = (bf16[768,256]{1,0:T(8,128)(2,1)S(1)}, bf16[768,256]{1,0:T(8,128)(2,1)S(1)}, u32[]{:S(2)}, u32[]{:S(2)}) collective-permute-start(bf16[768,256]{1,0:T(8,128)(2,1)S(1)} %shard_map.99.refs_0_), channel_id=1, source_target_pairs={{0,2},{1,3},{2,0},{3,1},{4,6},{5,7},{6,4},{7,5},{8,10},{9,11},{10,... | collective-permute-start | bytes 1179656 | tf_op jit(solution)/shard_map/ppermute | solution.py:312
  196.0 14.5 %collective-permute-start.46 = (bf16[768,256]{1,0:T(8,128)(2,1)S(1)}, bf16[768,256]{1,0:T(8,128)(2,1)S(1)}, u32[]{:S(2)}, u32[]{:S(2)}) collective-permute-start(bf16[768,256]{1,0:T(8,128)(2,1)S(1)} %shard_map.99.refs_0_), channel_id=1, source_target_pairs={{0,1},{1,0},{2,3},{3,2},{4,5},{5,4},{6,7},{7,6},{8,9},{9,8},{10,11... | collective-permute-start | bytes 1179656 | tf_op jit(solution)/shard_map/ppermute | solution.py:312
  196.0 15.0 %collective-permute-start.48 = (bf16[768,256]{1,0:T(8,128)(2,1)S(1)}, bf16[768,256]{1,0:T(8,128)(2,1)S(1)}, u32[]{:S(2)}, u32[]{:S(2)}) collective-permute-start(bf16[768,256]{1,0:T(8,128)(2,1)S(1)} %collective-permute-done.47.refs_2_), channel_id=1, source_target_pairs={{0,1},{1,0},{2,3},{3,2},{4,5},{5,4},{6,7},{7,6},{8,9},{9,8},{10,11... | collective-permute-start | bytes 1179656 | tf_op jit(solution)/shard_map/ppermute | solution.py:312
  (60 other events, 669.7 us)

commit v2 on v1

--- a/solution.py
+++ b/solution.py
@@ -93,13 +93,17 @@
             out_refs[2 * o + 1][:, j * size : (j + 1) * size] = jnp.where(odd, low, high)
 
 
-def decay_kernel(flags_ref, tok_ref, gate_ref, rate_ref, out_ref, *, hp):
+def decay_kernel(flags_ref, tok_ref, gate_ref, far_ref, rate_ref, out_ref, *, hp):
+    heads = gate_ref.shape[1]
+    gates = [ref[k] for k in range(gate_ref.shape[0]) for ref in (gate_ref, far_ref)]
+    gate = jnp.concatenate(gates, axis=1).astype(F32)
+    gate = jnp.concatenate([gate, jnp.zeros((16 - heads, gate.shape[1]), F32)], axis=0).astype(BF)
     logit = lax.dot_general(
-        gate_ref[...], tok_ref[...], (((1,), (1,)), ((), ())), preferred_element_type=F32
+        gate, tok_ref[...], (((1,), (1,)), ((), ())), preferred_element_type=F32
     )
-    logit = logit[0 : rate_ref.shape[0], :]
+    logit = logit[0:8, :]
     soft = jnp.maximum(logit, 0.0) + jnp.log1p(jnp.exp(-jnp.abs(logit)))
-    run = -rate_ref[...] * soft
+    run = -rate_ref[:, 0:1] * soft
     lane = lax.broadcasted_iota(jnp.int32, run.shape, 1)
     step = 1
     while step < run.shape[1]:
@@ -253,11 +257,6 @@
             out_refs[n][lo:hi, :] = normed.astype(BF)
 
 
-def join_kernel(a_ref, b_ref, out_ref):
-    out_ref[:, : a_ref.shape[1]] = a_ref[...]
-    out_ref[:, a_ref.shape[1] :] = b_ref[...]
-
-
 def out_kernel(flags_ref, weight_ref, *refs, n_tp, heads, hp, head, flags, size, acc):
     out_ref = refs[-1]
     normed = refs[: len(refs) - 1 - acc]
@@ -295,6 +294,7 @@
     n_seq, n_tp = mesh.shape["seq"], mesh.shape["tp"]
     planes = n_seq // 2
     hops = n_seq // 4 - 1
+    chunks = 3
     bits = [1 << b for b in reversed(range((n_tp - 1).bit_length()))]
     steps = sorted(range(1, planes), key=lambda k: (k % 2 == 0, min(k, planes - k), k))
 
@@ -332,9 +332,7 @@
         rows = key_weight.shape[0]
 
         tile = tok_rows // n_tp
-        last = tile // 3 if tile % 48 == 0 else tile // 2
-        sizes = (tile - last, last)
-        chunks = len(sizes)
+        sizes = (tile // chunks,) * chunks
         mine = turn(where, tokens, planes, rows, tile, sizes, 1, 61)
         pieces = [None] * (n_tp * chunks)
         for c in range(chunks):
@@ -352,6 +350,7 @@
             ],
             (flags, key_weight, value_weight, query_weight),
             cost(1e6, key_weight.size * 12),
+            61,
         )
 
         def gather(g):
@@ -375,15 +374,11 @@
                 jnp.where(half == 0, gate_z, gate_zy),
                 jnp.where(half == 0, gate_zy, gate_z),
             )
-        gate_all = jnp.concatenate([gate_z, gate_zy], axis=2)
-        gate_all = gate_all.transpose(1, 0, 2).reshape(heads, width)
-        rows8 = -(-heads // 8) * 8
-        gate_all = jnp.pad(gate_all, ((0, 2 * rows8 - heads), (0, 0)))
-        rate = jnp.pad(decay_rate[:, None], ((0, rows8 - heads), (0, 0)))
+        rate = jnp.broadcast_to(jnp.pad(decay_rate, (0, 8 - heads))[:, None], (8, 128))
         within = call(
             functools.partial(decay_kernel, hp=hp),
-            jax.ShapeDtypeStruct((rows8, tok_rows), F32),
-            (flags, own_tokens, gate_all, rate),
+            jax.ShapeDtypeStruct((8, tok_rows), F32),
+            (flags, own_tokens, gate_z, gate_zy, rate),
             cost(64 * tok_rows * width, 2 * tok_rows * width),
         )
         within_far = lax.ppermute(within, "seq", pair_swap)
@@ -463,13 +458,7 @@
             if head < hp - 1:
                 normed, normed_far = mix((0, 1))
                 back = lax.ppermute(normed_far, "seq", pair_swap)
-                both = call(
-                    join_kernel,
-                    jax.ShapeDtypeStruct((tok_rows, 2 * size), BF),
-                    (normed, back),
-                    cost(1e6, 8 * tok_rows * size),
-                )
-                both = over_tp(both)
+                both = over_tp(normed) + over_tp(back)
                 acc = [out(both, head, (0, 1), False)]
             else:
                 (normed_far,) = mix((1,))

time: 217 us -> 215 us (level)
  local copies, waits for them, and re-layouts: 12.9 us -> 4.14 us
  starting transfers between devices: 58.3 us -> 64.2 us
  Pallas kernels: 44.6 us -> 41.9 us
  waiting for transfers between devices: 99.6 us -> 102 us
    ppermute x15 -> x21, waiting for transfers between devices: 9.02 us -> 23.7 us  [over_tp(): lax.ppermute(v, 'tp', swap)]
    ppermute x2, waiting for transfers between devices: 15.9 us -> 1.89 us  [body(): far = lax.ppermute(local, 'seq', half_swap)]
    unnamed x70 -> x22, local copies, waits for them, and re-layouts: 10.7 us -> 3.33 us
    ppermute x2 -> x3, waiting for transfers between devices: 23.4 us -> 30.7 us  [body(): got = over_tp(lax.ppermute(mine[c], 'seq', pair_swap))]
    ppermute x3, waiting for transfers between devices: 7.11 us -> 0.01 us  [body(): gate_z = {k: lax.ppermute(gate, 'seq', from_plane(k)) for k in steps}]
    ppermute x15 -> x21, starting transfers between devices: 5.98 us -> 10.3 us  [over_tp(): lax.ppermute(v, 'tp', swap)]
    ppermute x1, waiting for transfers between devices: 0.01 us -> 3.25 us  [body(): within_far = lax.ppermute(within, 'seq', pair_swap)]
    ppermute x9, starting transfers between devices: 15.5 us -> 18.5 us  [gather(): got[k] = lax.ppermute(give if k % 2 else keep, 'seq', from_plane(k))]
  transfers between devices with their start and end apart: 49 -> 56, of which waited for: 14 -> 18; matrix products, arithmetic and copies ran while one was open for 1% -> 1% of each run, Pallas kernels for 17% -> 18%
where the time goes in v2:
time: 215 us; the launch traced here: 214 us
  waiting for transfers between devices  102 us (47%)
  starting transfers between devices  64.2 us (30%)
  Pallas kernels  41.9 us (19%)
  local copies, waits for them, and re-layouts  4.14 us (2%)
    pallas_call x18, Pallas kernels, call(): pl.pallas_call(kernel, out_shape=out_shape, in_specs=[VMEM] * len(args),...  32.2 us
    ppermute x9, waiting for transfers between devices, gather(): got[k] = lax.ppermute(give if k % 2 else keep, 'seq', from_plane(k))  32.1 us
    ppermute x3, waiting for transfers between devices, body(): got = over_tp(lax.ppermute(mine[c], 'seq', pair_swap))  30.7 us
    ppermute x21, waiting for transfers between devices, over_tp(): lax.ppermute(v, 'tp', swap)  23.7 us
    ppermute x9, starting transfers between devices, gather(): got[k] = lax.ppermute(give if k % 2 else keep, 'seq', from_plane(k))  18.5 us
    ppermute x12, starting transfers between devices, gather(): blocks += [got[k], lax.ppermute(got[k], 'seq', half_swap)]  12.3 us
    ppermute x21, starting transfers between devices, over_tp(): lax.ppermute(v, 'tp', swap)  10.3 us
    pallas_call x2, Pallas kernels, turn(): pl.pallas_call(functools.partial(turn_kernel, planes=planes, rows=rows, o...  9.64 us
  transfers between devices with their start and end apart: 56, of which 18 were waited for; matrix products, arithmetic and copies ran while one was open for 1% of the time, Pallas kernels for 18%

profile of v2, /device:TPU:0, one launch (start us, length us, event | category | flops | bytes accessed | tf_op | source)
XLA Modules:
  0.0 214.2 jit_solution(15083264478190817817)
XLA Ops:
  0.0 4.1 %collective-permute-start.27 = (bf16[4,512]{1,0:T(4,128)(2,1)}, bf16[4,512]{1,0:T(4,128)(2,1)S(1)}, u32[]{:S(2)}, u32[]{:S(2)}) collective-permute-start(bf16[4,512]{1,0:T(4,128)(2,1)} %bitcast.16), channel_id=1, source_target_pairs={{16,0},{20,4},{24,8},{28,12},{0,16},{4,20},{8,24},{12,28},{17,1},{... | collective-permute-start | bytes 12296 | tf_op jit(solution)/shard_map/ppermute | solution.py:369
  6.8 2.7 %shard_map.83 = (bf16[512,384]{1,0:T(8,128)(2,1)}, bf16[512,384]{1,0:T(8,128)(2,1)}, bf16[512,256]{1,0:T(8,128)(2,1)}, bf16[512,256]{1,0:T(8,128)(2,1)}, bf16[51...) custom-call(f32[8,128]{1,0:T(8,128)} %broadcast_in_dim.4.flags_ref, bf16[512,512]{1,0:T(8,128)(2,1)} %k_ref.1, ...), custom_call_target="tpu_custom_call" | custom-call | flops 1000000 | bytes 3145728 | tf_op jit(solution)/shard_map/pallas_call | solution.py:27
  20.7 8.1 %collective-permute-start.41 = (bf16[512,384]{1,0:T(8,128)(2,1)}, bf16[512,384]{1,0:T(8,128)(2,1)S(1)}, u32[]{:S(2)}, u32[]{:S(2)}) collective-permute-start(bf16[512,384]{1,0:T(8,128)(2,1)} %get-tuple-element.24), channel_id=1, source_target_pairs={{8,0},{12,4},{16,8},{20,12},{24,16},{28,20},{0,24},{4,28},{9,1},{1... | collective-permute-start | bytes 1179656 | tf_op jit(solution)/shard_map/ppermute | solution.py:360
  29.6 14.5 %collective-permute-done.15.refs_16_.refs_5_ = bf16[512,256]{1,0:T(8,128)(2,1)S(1)} collective-permute-done((bf16[512,256]{1,0:T(8,128)(2,1)}, bf16[512,256]{1,0:T(8,128)(2,1)S(1)}, u32[]{:S(2)}, u32[]{:S(2)}) %collective-permute-start.15) | collective-permute-done | bytes 262176 | tf_op jit(solution)/shard_map/ppermute | solution.py:360
  48.3 3.6 %shard_map.82 = (bf16[64,4096]{1,0:T(8,128)(2,1)}, bf16[64,4096]{1,0:T(8,128)(2,1)}, bf16[64,4096]{1,0:T(8,128)(2,1)}) custom-call(s32[4]{0:T(128)} %pad_add_fusion.where, bf16[768,4096]{1,0:T(8,128)(2,1)} %tok_ref.3), custom_call_target="tpu_custom_call" | custom-call | flops 1000000 | bytes 3145728 | tf_op jit(solution)/shard_map/pallas_call | solution.py:71
  52.4 16.8 %collective-permute-done.43.refs_5_.refs_16_ = bf16[512,384]{1,0:T(8,128)(2,1)S(1)} collective-permute-done((bf16[512,384]{1,0:T(8,128)(2,1)}, bf16[512,384]{1,0:T(8,128)(2,1)S(1)}, u32[]{:S(2)}, u32[]{:S(2)}) %collective-permute-start.43) | collective-permute-done | bytes 393248 | tf_op jit(solution)/shard_map/ppermute | solution.py:360
  73.5 10.7 %collective-permute-done.refs_0_ = bf16[64,4096]{1,0:T(8,128)(2,1)S(1)} collective-permute-done((bf16[64,4096]{1,0:T(8,128)(2,1)}, bf16[64,4096]{1,0:T(8,128)(2,1)S(1)}, u32[]{:S(2)}, u32[]{:S(2)}) %collective-permute-start) | collective-permute-done | bytes 524320 | tf_op jit(solution)/shard_map/ppermute | solution.py:339
  85.7 9.7 %collective-permute-done.1.refs_1_ = bf16[64,4096]{1,0:T(8,128)(2,1)S(1)} collective-permute-done((bf16[64,4096]{1,0:T(8,128)(2,1)}, bf16[64,4096]{1,0:T(8,128)(2,1)S(1)}, u32[]{:S(2)}, u32[]{:S(2)}) %collective-permute-start.1) | collective-permute-done | bytes 524320 | tf_op jit(solution)/shard_map/ppermute | solution.py:339
  95.5 10.2 %collective-permute-done.2.refs_2_ = bf16[64,4096]{1,0:T(8,128)(2,1)S(1)} collective-permute-done((bf16[64,4096]{1,0:T(8,128)(2,1)}, bf16[64,4096]{1,0:T(8,128)(2,1)S(1)}, u32[]{:S(2)}, u32[]{:S(2)}) %collective-permute-start.2) | collective-permute-done | bytes 524320 | tf_op jit(solution)/shard_map/ppermute | solution.py:339
  109.2 8.0 %collective-permute-done.44.refs_6_.refs_17_ = bf16[512,384]{1,0:T(8,128)(2,1)S(1)} collective-permute-done((bf16[512,384]{1,0:T(8,128)(2,1)S(1)}, bf16[512,384]{1,0:T(8,128)(2,1)S(1)}, u32[]{:S(2)}, u32[]{:S(2)}) %collective-permute-start.44) | collective-permute-done | bytes 393248 | tf_op jit(solution)/shard_map/ppermute | solution.py:363
  117.9 2.6 %collective-permute-done.7.refs_7_ = bf16[64,4096]{1,0:T(8,128)(2,1)S(1)} collective-permute-done((bf16[64,4096]{1,0:T(8,128)(2,1)S(1)}, bf16[64,4096]{1,0:T(8,128)(2,1)S(1)}, u32[]{:S(2)}, u32[]{:S(2)}) %collective-permute-start.7) | collective-permute-done | bytes 524320 | tf_op jit(solution)/shard_map/ppermute | solution.py:312
  120.5 9.3 %collective-permute-done.8.refs_8_ = bf16[64,4096]{1,0:T(8,128)(2,1)S(1)} collective-permute-done((bf16[64,4096]{1,0:T(8,128)(2,1)S(1)}, bf16[64,4096]{1,0:T(8,128)(2,1)S(1)}, u32[]{:S(2)}, u32[]{:S(2)}) %collective-permute-start.8) | collective-permute-done | bytes 524320 | tf_op jit(solution)/shard_map/ppermute | solution.py:312
  129.9 6.1 %shard_map.86.tok_ref.refs_0_ = bf16[768,4096]{1,0:T(8,128)(2,1)} custom-call(s32[4]{0:T(128)S(1)} %copy-done.8, bf16[768,4096]{1,0:T(8,128)(2,1)} %tok_ref.3), custom_call_target="tpu_custom_call" | custom-call | flops 1000000 | bytes 12582912 | tf_op jit(solution)/shard_map/pallas_call | solution.py:71
  136.0 2.8 %copy-done = bf16[768,4096]{1,0:T(8,128)(2,1)S(1)} copy-done((bf16[768,4096]{1,0:T(8,128)(2,1)S(1)}, bf16[768,4096]{1,0:T(8,128)(2,1)}, u32[]{:S(2)}) %copy-start) | copy-done | bytes 6291480
  141.6 2.8 %shard_map.88.own_ref.refs_0_ = bf16[768,256]{1,0:T(8,128)(2,1)S(1)} custom-call(f32[8,128]{1,0:T(8,128)S(1)} %copy-done.4, bf16[768,4096]{1,0:T(8,128)(2,1)S(1)} %copy-done.1, bf16[512,256]{1,0:T(8,128)(2,1)S(1)} %copy-done.5, bf16[512,256]{1,0:T(8,128)(2,1)S(1)} %collective-permute-done.12.refs_13_.refs_2_, ...), custom_call_target="tpu_custom_call" | custom-call | flops 1610612736 | bytes 6291456 | tf_op jit(solution)/shard_map/pallas_call | solution.py:27
  144.5 3.5 %shard_map.94.own_ref.refs_0_.refs_1_ = bf16[768,384]{1,0:T(8,128)(2,1)S(1)} custom-call(f32[8,128]{1,0:T(8,128)S(1)} %copy-done.4, bf16[768,4096]{1,0:T(8,128)(2,1)S(1)} %copy-done.1, bf16[512,384]{1,0:T(8,128)(2,1)S(1)} %copy-done.3, bf16[512,384]{1,0:T(8,128)(2,1)S(1)} %collective-permute-done.40.refs_2_.refs_13_, ...), custom_call_target="tpu_custom_call" | custom-call | flops 2415919104 | bytes 6291456 | tf_op jit(solution)/shard_map/pallas_call | solution.py:27
  148.6 3.3 %collective-permute-start.20 = (bf16[512,128]{1,0:T(8,128)(2,1)S(1)}, bf16[512,128]{1,0:T(8,128)(2,1)S(1)}, u32[]{:S(2)}, u32[]{:S(2)}) collective-permute-start(bf16[512,128]{1,0:T(8,128)(2,1)S(1)} %copy-done.9), channel_id=1, source_target_pairs={{8,0},{12,4},{16,8},{20,12},{24,16},{28,20},{0,24},{4,28},{9,1},{1... | collective-permute-start | bytes 393224 | tf_op jit(solution)/shard_map/ppermute | solution.py:360
  152.5 3.5 %shard_map.95.far_ref.refs_2_.refs_3_ = bf16[768,384]{1,0:T(8,128)(2,1)S(1)} custom-call(f32[8,128]{1,0:T(8,128)S(1)} %copy-done.4, bf16[64,4096]{1,0:T(8,128)(2,1)S(1)} %collective-permute-done.refs_0_, bf16[64,4096]{1,0:T(8,128)(2,1)S(1)} %collective-permute-done.1.refs_1_, bf16[64,4096]{1,0:T(8,128)(2,1)S(1)} %collective-permute-done.2.refs_2_, ...), custom_call_target="tpu_custom_call" | custom-call | flops 2415919104 | bytes 6291456 | tf_op jit(solution)/shard_map/pallas_call | solution.py:27
  156.0 3.2 %collective-permute-done.30.winp_ref.refs_2_.refs_5_ = f32[8,768]{1,0:T(8,128)S(1)} collective-permute-done((f32[8,768]{1,0:T(8,128)S(1)}, f32[8,768]{1,0:T(8,128)S(1)}, u32[]{:S(2)}, u32[]{:S(2)}) %collective-permute-start.30) | collective-permute-done | bytes 24608 | tf_op jit(solution)/shard_map/ppermute | solution.py:384
  161.5 2.7 %shard_map.84.far_ref.refs_0_ = bf16[768,256]{1,0:T(8,128)(2,1)S(1)} custom-call(f32[8,128]{1,0:T(8,128)S(1)} %copy-done.4, bf16[64,4096]{1,0:T(8,128)(2,1)S(1)} %collective-permute-done.refs_0_, bf16[64,4096]{1,0:T(8,128)(2,1)S(1)} %collective-permute-done.1.refs_1_, bf16[64,4096]{1,0:T(8,128)(2,1)S(1)} %collective-permute-done.2.refs_2_, ...), custom_call_target="tpu_custom_call" | custom-call | flops 1610612736 | bytes 6291456 | tf_op jit(solution)/shard_map/pallas_call | solution.py:27
  171.5 5.2 %collective-permute-start.48 = (f32[128,128]{1,0:T(8,128)S(1)}, f32[128,128]{1,0:T(8,128)S(1)}, u32[]{:S(2)}, u32[]{:S(2)}) collective-permute-start(f32[128,128]{1,0:T(8,128)S(1)} %shard_map.97), channel_id=1, source_target_pairs={{0,16},{4,20},{8,24},{12,28},{1,17},{5,21},{9,25},{13,29},{2,18},{... | collective-permute-start | bytes 196616 | tf_op jit(solution)/shard_map/ppermute | solution.py:433
  176.8 2.7 %collective-permute-start.32 = (f32[128,128]{1,0:T(8,128)S(1)}, f32[128,128]{1,0:T(8,128)S(1)}, u32[]{:S(2)}, u32[]{:S(2)}) collective-permute-start(f32[128,128]{1,0:T(8,128)S(1)} %shard_map.90), channel_id=1, source_target_pairs={{0,16},{4,20},{8,24},{12,28},{1,17},{5,21},{9,25},{13,29},{2,18},{... | collective-permute-start | bytes 196616 | tf_op jit(solution)/shard_map/ppermute | solution.py:433
  198.3 4.2 %collective-permute-done.50.refs_2_ = bf16[768,128]{1,0:T(8,128)(2,1)S(1)} collective-permute-done((bf16[768,128]{1,0:T(8,128)(2,1)S(1)}, bf16[768,128]{1,0:T(8,128)(2,1)S(1)}, u32[]{:S(2)}, u32[]{:S(2)}) %collective-permute-start.50) | collective-permute-done | bytes 196640 | tf_op jit(solution)/shard_map/ppermute | solution.py:312
  202.5 3.3 %collective-permute-done.54.refs_6_ = bf16[768,128]{1,0:T(8,128)(2,1)S(1)} collective-permute-done((bf16[768,128]{1,0:T(8,128)(2,1)S(1)}, bf16[768,128]{1,0:T(8,128)(2,1)S(1)}, u32[]{:S(2)}, u32[]{:S(2)}) %collective-permute-start.54) | collective-permute-done | bytes 196640 | tf_op jit(solution)/shard_map/ppermute | solution.py:312
  (137 shorter events, 70.1 us)
Async XLA Ops:
  11.1 17.7 %collective-permute-start.13 = (bf16[512,256]{1,0:T(8,128)(2,1)}, bf16[512,256]{1,0:T(8,128)(2,1)S(1)}, u32[]{:S(2)}, u32[]{:S(2)}) collective-permute-start(bf16[512,256]{1,0:T(8,128)(2,1)} %get-tuple-element.20), channel_id=1, source_target_pairs={{8,0},{12,4},{16,8},{20,12},{24,16},{28,20},{0,24},{4,28},{9,1},{1... | collective-permute-start | bytes 786440 | tf_op jit(solution)/shard_map/ppermute | solution.py:360
  13.3 30.8 %collective-permute-start.15 = (bf16[512,256]{1,0:T(8,128)(2,1)}, bf16[512,256]{1,0:T(8,128)(2,1)S(1)}, u32[]{:S(2)}, u32[]{:S(2)}) collective-permute-start(bf16[512,256]{1,0:T(8,128)(2,1)} %get-tuple-element.19.refs_12_.refs_1_), channel_id=1, source_target_pairs={{16,0},{20,4},{24,8},{28,12},{0,16},{4,20},{8,24},{12,28},{17,1},{... | collective-permute-start | bytes 786440 | tf_op jit(solution)/shard_map/ppermute | solution.py:360
  15.6 30.0 %collective-permute-start.12 = (bf16[512,256]{1,0:T(8,128)(2,1)}, bf16[512,256]{1,0:T(8,128)(2,1)S(1)}, u32[]{:S(2)}, u32[]{:S(2)}) collective-permute-start(bf16[512,256]{1,0:T(8,128)(2,1)} %get-tuple-element.19.refs_12_.refs_1_), channel_id=1, source_target_pairs={{0,4},{4,0},{8,12},{12,8},{16,20},{20,16},{24,28},{28,24},{1,5},{5... | collective-permute-start | bytes 786440 | tf_op jit(solution)/shard_map/ppermute | solution.py:363
  18.0 28.1 %collective-permute-start.45 = (bf16[512,384]{1,0:T(8,128)(2,1)}, bf16[512,384]{1,0:T(8,128)(2,1)S(1)}, u32[]{:S(2)}, u32[]{:S(2)}) collective-permute-start(bf16[512,384]{1,0:T(8,128)(2,1)} %get-tuple-element.24), channel_id=1, source_target_pairs={{24,0},{28,4},{0,8},{4,12},{8,16},{12,20},{16,24},{20,28},{25,1},{... | collective-permute-start | bytes 1179656 | tf_op jit(solution)/shard_map/ppermute | solution.py:360
  20.7 31.1 %collective-permute-start.41 = (bf16[512,384]{1,0:T(8,128)(2,1)}, bf16[512,384]{1,0:T(8,128)(2,1)S(1)}, u32[]{:S(2)}, u32[]{:S(2)}) collective-permute-start(bf16[512,384]{1,0:T(8,128)(2,1)} %get-tuple-element.24), channel_id=1, source_target_pairs={{8,0},{12,4},{16,8},{20,12},{24,16},{28,20},{0,24},{4,28},{9,1},{1... | collective-permute-start | bytes 1179656 | tf_op jit(solution)/shard_map/ppermute | solution.py:360
  28.8 40.4 %collective-permute-start.43 = (bf16[512,384]{1,0:T(8,128)(2,1)}, bf16[512,384]{1,0:T(8,128)(2,1)S(1)}, u32[]{:S(2)}, u32[]{:S(2)}) collective-permute-start(bf16[512,384]{1,0:T(8,128)(2,1)} %get-tuple-element.23.refs_1_.refs_12_), channel_id=1, source_target_pairs={{16,0},{20,4},{24,8},{28,12},{0,16},{4,20},{8,24},{12,28},{17,1},{... | collective-permute-start | bytes 1179656 | tf_op jit(solution)/shard_map/ppermute | solution.py:360
  44.1 25.1 %collective-permute-start.40 = (bf16[512,384]{1,0:T(8,128)(2,1)}, bf16[512,384]{1,0:T(8,128)(2,1)S(1)}, u32[]{:S(2)}, u32[]{:S(2)}) collective-permute-start(bf16[512,384]{1,0:T(8,128)(2,1)} %get-tuple-element.23.refs_1_.refs_12_), channel_id=1, source_target_pairs={{0,4},{4,0},{8,12},{12,8},{16,20},{20,16},{24,28},{28,24},{1,5},{5... | collective-permute-start | bytes 1179656 | tf_op jit(solution)/shard_map/ppermute | solution.py:363
  45.7 25.6 %collective-permute-start.18 = (bf16[512,256]{1,0:T(8,128)(2,1)S(1)}, bf16[512,256]{1,0:T(8,128)(2,1)S(1)}, u32[]{:S(2)}, u32[]{:S(2)}) collective-permute-start(bf16[512,256]{1,0:T(8,128)(2,1)S(1)} %collective-permute-done.17.refs_18_.refs_7_), channel_id=1, source_target_pairs={{0,4},{4,0},{8,12},{12,8},{16,20},{20,16},{24,28},{28,24},{1,5},{5... | collective-permute-start | bytes 786440 | tf_op jit(solution)/shard_map/ppermute | solution.py:363
  46.2 25.2 %collective-permute-start.14 = (bf16[512,256]{1,0:T(8,128)(2,1)S(1)}, bf16[512,256]{1,0:T(8,128)(2,1)}, u32[]{:S(2)}, u32[]{:S(2)}) collective-permute-start(bf16[512,256]{1,0:T(8,128)(2,1)S(1)} %collective-permute-done.13.refs_14_.refs_3_), channel_id=1, source_target_pairs={{0,4},{4,0},{8,12},{12,8},{16,20},{20,16},{24,28},{28,24},{1,5},{5... | collective-permute-start | bytes 786440 | tf_op jit(solution)/shard_map/ppermute | solution.py:363
  51.9 21.0 %collective-permute-start.16 = (bf16[512,256]{1,0:T(8,128)(2,1)S(1)}, bf16[512,256]{1,0:T(8,128)(2,1)S(1)}, u32[]{:S(2)}, u32[]{:S(2)}) collective-permute-start(bf16[512,256]{1,0:T(8,128)(2,1)S(1)} %collective-permute-done.15.refs_16_.refs_5_), channel_id=1, source_target_pairs={{0,4},{4,0},{8,12},{12,8},{16,20},{20,16},{24,28},{28,24},{1,5},{5... | collective-permute-start | bytes 786440 | tf_op jit(solution)/shard_map/ppermute | solution.py:363
  69.3 26.2 %collective-permute-start.1 = (bf16[64,4096]{1,0:T(8,128)(2,1)}, bf16[64,4096]{1,0:T(8,128)(2,1)S(1)}, u32[]{:S(2)}, u32[]{:S(2)}) collective-permute-start(bf16[64,4096]{1,0:T(8,128)(2,1)} %get-tuple-element.17), channel_id=1, source_target_pairs={{0,8},{4,12},{8,0},{12,4},{16,24},{20,28},{24,16},{28,20},{1,9},{5... | collective-permute-start | bytes 1572872 | tf_op jit(solution)/shard_map/ppermute | solution.py:339
  71.3 34.4 %collective-permute-start.2 = (bf16[64,4096]{1,0:T(8,128)(2,1)}, bf16[64,4096]{1,0:T(8,128)(2,1)S(1)}, u32[]{:S(2)}, u32[]{:S(2)}) collective-permute-start(bf16[64,4096]{1,0:T(8,128)(2,1)} %get-tuple-element.18), channel_id=1, source_target_pairs={{0,8},{4,12},{8,0},{12,4},{16,24},{20,28},{24,16},{28,20},{1,9},{5... | collective-permute-start | bytes 1572872 | tf_op jit(solution)/shard_map/ppermute | solution.py:339
  71.4 35.8 %collective-permute-start.46 = (bf16[512,384]{1,0:T(8,128)(2,1)S(1)}, bf16[512,384]{1,0:T(8,128)(2,1)S(1)}, u32[]{:S(2)}, u32[]{:S(2)}) collective-permute-start(bf16[512,384]{1,0:T(8,128)(2,1)S(1)} %collective-permute-done.45.refs_7_.refs_18_), channel_id=1, source_target_pairs={{0,4},{4,0},{8,12},{12,8},{16,20},{20,16},{24,28},{28,24},{1,5},{5... | collective-permute-start | bytes 1179656 | tf_op jit(solution)/shard_map/ppermute | solution.py:363
  72.9 34.8 %collective-permute-start.42 = (bf16[512,384]{1,0:T(8,128)(2,1)S(1)}, bf16[512,384]{1,0:T(8,128)(2,1)S(1)}, u32[]{:S(2)}, u32[]{:S(2)}) collective-permute-start(bf16[512,384]{1,0:T(8,128)(2,1)S(1)} %collective-permute-done.41.refs_3_.refs_14_), channel_id=1, source_target_pairs={{0,4},{4,0},{8,12},{12,8},{16,20},{20,16},{24,28},{28,24},{1,5},{5... | collective-permute-start | bytes 1179656 | tf_op jit(solution)/shard_map/ppermute | solution.py:363
  84.3 33.0 %collective-permute-start.6 = (bf16[64,4096]{1,0:T(8,128)(2,1)S(1)}, bf16[64,4096]{1,0:T(8,128)(2,1)S(1)}, u32[]{:S(2)}, u32[]{:S(2)}) collective-permute-start(bf16[64,4096]{1,0:T(8,128)(2,1)S(1)} %collective-permute-done.refs_0_), channel_id=1, source_target_pairs={{0,2},{1,3},{2,0},{3,1},{4,6},{5,7},{6,4},{7,5},{8,10},{9,11},{10,... | collective-permute-start | bytes 1572872 | tf_op jit(solution)/shard_map/ppermute | solution.py:312
  95.5 22.3 %collective-permute-start.3 = (bf16[64,4096]{1,0:T(8,128)(2,1)S(1)}, bf16[64,4096]{1,0:T(8,128)(2,1)S(1)}, u32[]{:S(2)}, u32[]{:S(2)}) collective-permute-start(bf16[64,4096]{1,0:T(8,128)(2,1)S(1)} %collective-permute-done.refs_0_), channel_id=1, source_target_pairs={{0,1},{1,0},{2,3},{3,2},{4,5},{5,4},{6,7},{7,6},{8,9},{9,8},{10,11... | collective-permute-start | bytes 1572872 | tf_op jit(solution)/shard_map/ppermute | solution.py:312
  107.2 22.6 %collective-permute-start.8 = (bf16[64,4096]{1,0:T(8,128)(2,1)S(1)}, bf16[64,4096]{1,0:T(8,128)(2,1)S(1)}, u32[]{:S(2)}, u32[]{:S(2)}) collective-permute-start(bf16[64,4096]{1,0:T(8,128)(2,1)S(1)} %collective-permute-done.2.refs_2_), channel_id=1, source_target_pairs={{0,2},{1,3},{2,0},{3,1},{4,6},{5,7},{6,4},{7,5},{8,10},{9,11},{10,... | collective-permute-start | bytes 1572872 | tf_op jit(solution)/shard_map/ppermute | solution.py:312
  117.3 30.7 %collective-permute-start.4 = (bf16[64,4096]{1,0:T(8,128)(2,1)S(1)}, bf16[64,4096]{1,0:T(8,128)(2,1)S(1)}, u32[]{:S(2)}, u32[]{:S(2)}) collective-permute-start(bf16[64,4096]{1,0:T(8,128)(2,1)S(1)} %collective-permute-done.1.refs_1_), channel_id=1, source_target_pairs={{0,1},{1,0},{2,3},{3,2},{4,5},{5,4},{6,7},{7,6},{8,9},{9,8},{10,11... | collective-permute-start | bytes 1572872 | tf_op jit(solution)/shard_map/ppermute | solution.py:312
  117.3 31.3 %collective-permute-start.5 = (bf16[64,4096]{1,0:T(8,128)(2,1)S(1)}, bf16[64,4096]{1,0:T(8,128)(2,1)S(1)}, u32[]{:S(2)}, u32[]{:S(2)}) collective-permute-start(bf16[64,4096]{1,0:T(8,128)(2,1)S(1)} %collective-permute-done.2.refs_2_), channel_id=1, source_target_pairs={{0,1},{1,0},{2,3},{3,2},{4,5},{5,4},{6,7},{7,6},{8,9},{9,8},{10,11... | collective-permute-start | bytes 1572872 | tf_op jit(solution)/shard_map/ppermute | solution.py:312
  117.8 34.1 %collective-permute-start.9 = (bf16[64,4096]{1,0:T(8,128)(2,1)S(1)}, bf16[64,4096]{1,0:T(8,128)(2,1)S(1)}, u32[]{:S(2)}, u32[]{:S(2)}) collective-permute-start(bf16[64,4096]{1,0:T(8,128)(2,1)S(1)} %collective-permute-done.6.refs_6_), channel_id=1, source_target_pairs={{0,1},{1,0},{2,3},{3,2},{4,5},{5,4},{6,7},{7,6},{8,9},{9,8},{10,11... | collective-permute-start | bytes 1572872 | tf_op jit(solution)/shard_map/ppermute | solution.py:312
  120.5 31.4 %collective-permute-start.10 = (bf16[64,4096]{1,0:T(8,128)(2,1)S(1)}, bf16[64,4096]{1,0:T(8,128)(2,1)S(1)}, u32[]{:S(2)}, u32[]{:S(2)}) collective-permute-start(bf16[64,4096]{1,0:T(8,128)(2,1)S(1)} %collective-permute-done.7.refs_7_), channel_id=1, source_target_pairs={{0,1},{1,0},{2,3},{3,2},{4,5},{5,4},{6,7},{7,6},{8,9},{9,8},{10,11... | collective-permute-start | bytes 1572872 | tf_op jit(solution)/shard_map/ppermute | solution.py:312
  129.8 22.7 %collective-permute-start.11 = (bf16[64,4096]{1,0:T(8,128)(2,1)S(1)}, bf16[64,4096]{1,0:T(8,128)(2,1)S(1)}, u32[]{:S(2)}, u32[]{:S(2)}) collective-permute-start(bf16[64,4096]{1,0:T(8,128)(2,1)S(1)} %collective-permute-done.8.refs_8_), channel_id=1, source_target_pairs={{0,1},{1,0},{2,3},{3,2},{4,5},{5,4},{6,7},{7,6},{8,9},{9,8},{10,11... | collective-permute-start | bytes 1572872 | tf_op jit(solution)/shard_map/ppermute | solution.py:312
  148.0 17.5 %collective-permute-start.24 = (bf16[512,128]{1,0:T(8,128)(2,1)S(1)}, bf16[512,128]{1,0:T(8,128)(2,1)S(1)}, u32[]{:S(2)}, u32[]{:S(2)}) collective-permute-start(bf16[512,128]{1,0:T(8,128)(2,1)S(1)} %copy-done.9), channel_id=1, source_target_pairs={{24,0},{28,4},{0,8},{4,12},{8,16},{12,20},{16,24},{20,28},{25,1},{... | collective-permute-start | bytes 393224 | tf_op jit(solution)/shard_map/ppermute | solution.py:360
  148.6 18.4 %collective-permute-start.20 = (bf16[512,128]{1,0:T(8,128)(2,1)S(1)}, bf16[512,128]{1,0:T(8,128)(2,1)S(1)}, u32[]{:S(2)}, u32[]{:S(2)}) collective-permute-start(bf16[512,128]{1,0:T(8,128)(2,1)S(1)} %copy-done.9), channel_id=1, source_target_pairs={{8,0},{12,4},{16,8},{20,12},{24,16},{28,20},{0,24},{4,28},{9,1},{1... | collective-permute-start | bytes 393224 | tf_op jit(solution)/shard_map/ppermute | solution.py:360
  (43 other events, 582.7 us)

commit v3 on v2

--- a/solution.py
+++ b/solution.py
@@ -82,21 +82,48 @@
     )(where, tokens)
 
 
-def pack_kernel(flags_ref, k_ref, v_ref, q_ref, *out_refs, groups, size, hp):
+def gate_rows(rows):
+    wide = min(rows, 256)
+    return rows // wide, wide
+
+
+def pack_kernel(flags_ref, k_ref, v_ref, q_ref, gate_ref, *out_refs, groups, size, hp):
+    rows = k_ref.shape[0]
+    parts, wide = gate_rows(rows)
+    gate = gate_ref[...].astype(F32)
+    tail = jnp.concatenate([gate[:, p * wide : (p + 1) * wide] for p in range(parts)], axis=0)
+    below = out_refs[0].shape[0] - rows
+    if tail.shape[0] < below:
+        tail = jnp.concatenate([tail, jnp.zeros((below - tail.shape[0], wide), F32)], axis=0)
+    for out_ref in out_refs[:2]:
+        rest = out_ref.shape[1] - wide
+        out_ref[rows:, :] = jnp.concatenate([tail, jnp.zeros((below, rest), F32)], axis=1).astype(BF)
     refs = {"k": k_ref, "v": v_ref, "q": q_ref}
-    odd = flag(flags_ref, 1, (k_ref.shape[0], size))
+    odd = flag(flags_ref, 1, (rows, size))
     for o, (head, names) in enumerate(groups):
         for j, n in enumerate(names):
             low = refs[n][:, head * size : (head + 1) * size]
             high = refs[n][:, (hp + head) * size : (hp + head + 1) * size]
-            out_refs[2 * o][:, j * size : (j + 1) * size] = jnp.where(odd, high, low)
-            out_refs[2 * o + 1][:, j * size : (j + 1) * size] = jnp.where(odd, low, high)
-
-
-def decay_kernel(flags_ref, tok_ref, gate_ref, far_ref, rate_ref, out_ref, *, hp):
-    heads = gate_ref.shape[1]
-    gates = [ref[k] for k in range(gate_ref.shape[0]) for ref in (gate_ref, far_ref)]
-    gate = jnp.concatenate(gates, axis=1).astype(F32)
+            out_refs[2 * o][0:rows, j * size : (j + 1) * size] = jnp.where(odd, high, low)
+            out_refs[2 * o + 1][0:rows, j * size : (j + 1) * size] = jnp.where(odd, low, high)
+
+
+def decay_kernel(flags_ref, tok_ref, rate_ref, *refs, hp, rows):
+    block_refs, out_ref = refs[:-1], refs[-1]
+    heads = 2 * hp
+    parts, wide = gate_rows(rows)
+    gates = []
+    for block_ref in block_refs:
+        tail = block_ref[rows:, 0:wide].astype(F32)
+        gates.append(
+            jnp.concatenate([tail[p * heads : (p + 1) * heads] for p in range(parts)], axis=1)
+        )
+    if rows % 128:
+        second = flag(flags_ref, 0, gates[0].shape)
+        for i in range(0, len(gates), 2):
+            a, b = gates[i], gates[i + 1]
+            gates[i], gates[i + 1] = jnp.where(second, b, a), jnp.where(second, a, b)
+    gate = jnp.concatenate(gates, axis=1)
     gate = jnp.concatenate([gate, jnp.zeros((16 - heads, gate.shape[1]), F32)], axis=0).astype(BF)
     logit = lax.dot_general(
         gate, tok_ref[...], (((1,), (1,)), ((), ())), preferred_element_type=F32
@@ -116,9 +143,8 @@
     out_ref[hp : 2 * hp, :] = jnp.where(odd, low, high)
 
 
-def project_kernel(flags_ref, *refs, parts, n_tp):
+def project_kernel(flags_ref, *refs, parts, n_tp, rows):
     tok_refs, block_refs, out_ref = refs[:parts], refs[parts:-1], refs[-1]
-    rows = block_refs[0].shape[0]
     cols = out_ref.shape[1]
     tok_rows = out_ref.shape[0]
     tile = tok_rows // n_tp
@@ -127,7 +153,9 @@
         acc = None
         for i, block_ref in enumerate(block_refs):
             part = jnp.dot(
-                pick(slice(i * rows, (i + 1) * rows)), block_ref[...], preferred_element_type=F32
+                pick(slice(i * rows, (i + 1) * rows)),
+                block_ref[0:rows, :],
+                preferred_element_type=F32,
             )
             acc = part if acc is None else acc + part
         return acc
@@ -157,13 +185,16 @@
 def project(flags, first, toks, blocks, n_tp):
     tok_rows = sum(t.shape[0] for t in toks)
     width, cols = toks[0].shape[1], blocks[0].shape[1]
-    if blocks[0].shape[0] % 128:
+    rows = width // len(blocks)
+    if rows % 128:
+        blocks = [b[:rows] for b in blocks]
         blocks = [
             jnp.concatenate([jnp.where(first, a, b), jnp.where(first, b, a)], axis=0)
             for a, b in zip(blocks[0::2], blocks[1::2])
         ]
+        rows = 2 * rows
     return call(
-        functools.partial(project_kernel, parts=len(toks), n_tp=n_tp),
+        functools.partial(project_kernel, parts=len(toks), n_tp=n_tp, rows=rows),
         jax.ShapeDtypeStruct((tok_rows, cols), BF),
         (flags, *toks, *blocks),
         cost(2 * tok_rows * width * max(cols, 256), 2 * tok_rows * width),
@@ -341,14 +372,15 @@
                 pieces[i * chunks + c] = got[i]
         (own_tokens,) = turn(where, tokens, planes, rows, 0, (tok_rows,), 0, 52)
 
+        below = -(-heads * gate_rows(rows)[0] // 8) * 8
         packed = call(
             functools.partial(pack_kernel, groups=groups, size=size, hp=hp),
             [
-                jax.ShapeDtypeStruct((rows, len(names) * size), BF)
-                for _, names in groups
+                jax.ShapeDtypeStruct((rows + (0 if g else below), len(names) * size), BF)
+                for g, (_, names) in enumerate(groups)
                 for _ in (0, 1)
             ],
-            (flags, key_weight, value_weight, query_weight),
+            (flags, key_weight, value_weight, query_weight, gate_weight.T),
             cost(1e6, key_weight.size * 12),
             61,
         )
@@ -365,20 +397,11 @@
 
         gathered = [gather(g) for g in range(len(groups))]
 
-        gate = gate_weight.T
-        gate_z = {k: lax.ppermute(gate, "seq", from_plane(k)) for k in steps}
-        gate_z = jnp.stack([gate] + [gate_z[k] for k in range(1, planes)])
-        gate_zy = lax.ppermute(gate_z, "seq", half_swap)
-        if rows % 128:
-            gate_z, gate_zy = (
-                jnp.where(half == 0, gate_z, gate_zy),
-                jnp.where(half == 0, gate_zy, gate_z),
-            )
         rate = jnp.broadcast_to(jnp.pad(decay_rate, (0, 8 - heads))[:, None], (8, 128))
         within = call(
-            functools.partial(decay_kernel, hp=hp),
+            functools.partial(decay_kernel, hp=hp, rows=rows),
             jax.ShapeDtypeStruct((8, tok_rows), F32),
-            (flags, own_tokens, gate_z, gate_zy, rate),
+            (flags, own_tokens, rate, *gathered[0]),
             cost(64 * tok_rows * width, 2 * tok_rows * width),
         )
         within_far = lax.ppermute(within, "seq", pair_swap)

time: 215 us -> 220 us (1.023)
  waiting for transfers between devices: 102 us -> 120 us
  starting transfers between devices: 64.2 us -> 54.9 us
    ppermute x9, waiting for transfers between devices: 32.1 us -> 43.8 us  [gather(): got[k] = lax.ppermute(give if k % 2 else keep, 'seq', from_plane(k))]
    ppermute x12, waiting for transfers between devices: 8.56 us -> 19.2 us  [gather(): blocks += [got[k], lax.ppermute(got[k], 'seq', half_swap)]]
    ppermute x4 -> x0, starting transfers between devices: 7.68 us -> none  [the longest x3 6.09 us: body(): gate_z = {k: lax.ppermute(gate, 'seq', from_plane(k)) for k in steps}]
    ppermute x3, waiting for transfers between devices: 30.7 us -> 23.5 us  [body(): got = over_tp(lax.ppermute(mine[c], 'seq', pair_swap))]
    ppermute x9, starting transfers between devices: 18.5 us -> 13.3 us  [gather(): got[k] = lax.ppermute(give if k % 2 else keep, 'seq', from_plane(k))]
    ppermute x21, waiting for transfers between devices: 23.7 us -> 28.7 us  [over_tp(): lax.ppermute(v, 'tp', swap)]
    ppermute x12, starting transfers between devices: 12.3 us -> 16.4 us  [gather(): blocks += [got[k], lax.ppermute(got[k], 'seq', half_swap)]]
  transfers between devices with their start and end apart: 56 -> 52, of which waited for: 18 -> 21; matrix products, arithmetic and copies ran while one was open for 1% -> 0% of each run, Pallas kernels for 18% -> 16%
where the time goes in v3:
time: 220 us
  waiting for transfers between devices  120 us (55%)
  starting transfers between devices  54.9 us (25%)
  Pallas kernels  40 us (18%)
  local copies, waits for them, and re-layouts  4.53 us (2%)
    ppermute x9, waiting for transfers between devices, gather(): got[k] = lax.ppermute(give if k % 2 else keep, 'seq', from_plane(k))  43.8 us
    pallas_call x18, Pallas kernels, call(): pl.pallas_call(kernel, out_shape=out_shape, in_specs=[VMEM] * len(args),...  30.3 us
    ppermute x21, waiting for transfers between devices, over_tp(): lax.ppermute(v, 'tp', swap)  28.7 us
    ppermute x3, waiting for transfers between devices, body(): got = over_tp(lax.ppermute(mine[c], 'seq', pair_swap))  23.5 us
    ppermute x12, waiting for transfers between devices, gather(): blocks += [got[k], lax.ppermute(got[k], 'seq', half_swap)]  19.2 us
    ppermute x12, starting transfers between devices, gather(): blocks += [got[k], lax.ppermute(got[k], 'seq', half_swap)]  16.4 us
    ppermute x9, starting transfers between devices, gather(): got[k] = lax.ppermute(give if k % 2 else keep, 'seq', from_plane(k))  13.3 us
    ppermute x21, starting transfers between devices, over_tp(): lax.ppermute(v, 'tp', swap)  10.3 us
  transfers between devices with their start and end apart: 52, of which 21 were waited for; matrix products, arithmetic and copies ran while one was open for 0% of the time, Pallas kernels for 16%

profile of v3, /device:TPU:0, one launch (start us, length us, event | category | flops | bytes accessed | tf_op | source)
XLA Modules:
  0.0 220.0 jit_solution(1057928443900583588)
XLA Ops:
  3.4 3.1 %collective-permute-start.17 = (bf16[512,256]{1,0:T(8,128)(2,1)}, bf16[512,256]{1,0:T(8,128)(2,1)S(1)}, u32[]{:S(2)}, u32[]{:S(2)}) collective-permute-start(bf16[512,256]{1,0:T(8,128)(2,1)} %get-tuple-element.20), channel_id=1, source_target_pairs={{24,0},{28,4},{0,8},{4,12},{8,16},{12,20},{16,24},{20,28},{25,1},{... | collective-permute-start | bytes 786440 | tf_op jit(solution)/shard_map/ppermute | solution.py:392
  11.5 4.4 %collective-permute-done.17.refs_18_.refs_7_ = bf16[512,256]{1,0:T(8,128)(2,1)S(1)} collective-permute-done((bf16[512,256]{1,0:T(8,128)(2,1)}, bf16[512,256]{1,0:T(8,128)(2,1)S(1)}, u32[]{:S(2)}, u32[]{:S(2)}) %collective-permute-start.17) | collective-permute-done | bytes 262176 | tf_op jit(solution)/shard_map/ppermute | solution.py:392
  17.7 11.6 %collective-permute-done.13.refs_14_.refs_3_ = bf16[512,256]{1,0:T(8,128)(2,1)S(1)} collective-permute-done((bf16[512,256]{1,0:T(8,128)(2,1)}, bf16[512,256]{1,0:T(8,128)(2,1)S(1)}, u32[]{:S(2)}, u32[]{:S(2)}) %collective-permute-start.13) | collective-permute-done | bytes 262176 | tf_op jit(solution)/shard_map/ppermute | solution.py:392
  31.2 3.6 %shard_map.82 = (bf16[64,4096]{1,0:T(8,128)(2,1)}, bf16[64,4096]{1,0:T(8,128)(2,1)}, bf16[64,4096]{1,0:T(8,128)(2,1)}) custom-call(s32[4]{0:T(128)} %pad_add_fusion.where, bf16[768,4096]{1,0:T(8,128)(2,1)} %tok_ref.3), custom_call_target="tpu_custom_call" | custom-call | flops 1000000 | bytes 3145728 | tf_op jit(solution)/shard_map/pallas_call | solution.py:71
  34.8 22.8 %collective-permute-done.15.refs_16_.refs_5_ = bf16[512,256]{1,0:T(8,128)(2,1)S(1)} collective-permute-done((bf16[512,256]{1,0:T(8,128)(2,1)}, bf16[512,256]{1,0:T(8,128)(2,1)S(1)}, u32[]{:S(2)}, u32[]{:S(2)}) %collective-permute-start.15) | collective-permute-done | bytes 262176 | tf_op jit(solution)/shard_map/ppermute | solution.py:392
  61.3 4.9 %collective-permute-done.29.refs_4_.refs_5_.refs_16_ = bf16[520,384]{1,0:T(8,128)(2,1)S(1)} collective-permute-done((bf16[520,384]{1,0:T(8,128)(2,1)}, bf16[520,384]{1,0:T(8,128)(2,1)S(1)}, u32[]{:S(2)}, u32[]{:S(2)}) %collective-permute-start.29) | collective-permute-done | bytes 399392 | tf_op jit(solution)/shard_map/ppermute | solution.py:392
  67.7 4.1 %collective-permute-done.26.refs_1_.refs_2_.refs_13_ = bf16[520,384]{1,0:T(8,128)(2,1)S(1)} collective-permute-done((bf16[520,384]{1,0:T(8,128)(2,1)S(1)}, bf16[520,384]{1,0:T(8,128)(2,1)S(1)}, u32[]{:S(2)}, u32[]{:S(2)}) %collective-permute-start.26) | collective-permute-done | bytes 399392 | tf_op jit(solution)/shard_map/ppermute | solution.py:395
  73.3 4.1 %collective-permute-done.refs_0_ = bf16[64,4096]{1,0:T(8,128)(2,1)S(1)} collective-permute-done((bf16[64,4096]{1,0:T(8,128)(2,1)}, bf16[64,4096]{1,0:T(8,128)(2,1)S(1)}, u32[]{:S(2)}, u32[]{:S(2)}) %collective-permute-start) | collective-permute-done | bytes 524320 | tf_op jit(solution)/shard_map/ppermute | solution.py:370
  79.0 9.7 %collective-permute-done.1.refs_1_ = bf16[64,4096]{1,0:T(8,128)(2,1)S(1)} collective-permute-done((bf16[64,4096]{1,0:T(8,128)(2,1)}, bf16[64,4096]{1,0:T(8,128)(2,1)S(1)}, u32[]{:S(2)}, u32[]{:S(2)}) %collective-permute-start.1) | collective-permute-done | bytes 524320 | tf_op jit(solution)/shard_map/ppermute | solution.py:370
  90.2 9.6 %collective-permute-done.2.refs_2_ = bf16[64,4096]{1,0:T(8,128)(2,1)S(1)} collective-permute-done((bf16[64,4096]{1,0:T(8,128)(2,1)}, bf16[64,4096]{1,0:T(8,128)(2,1)S(1)}, u32[]{:S(2)}, u32[]{:S(2)}) %collective-permute-start.2) | collective-permute-done | bytes 524320 | tf_op jit(solution)/shard_map/ppermute | solution.py:370
  102.8 5.2 %collective-permute-done.16.refs_17_.refs_6_ = bf16[512,256]{1,0:T(8,128)(2,1)S(1)} collective-permute-done((bf16[512,256]{1,0:T(8,128)(2,1)S(1)}, bf16[512,256]{1,0:T(8,128)(2,1)S(1)}, u32[]{:S(2)}, u32[]{:S(2)}) %collective-permute-start.16) | collective-permute-done | bytes 262176 | tf_op jit(solution)/shard_map/ppermute | solution.py:395
  111.6 8.2 %collective-permute-done.30.refs_5_.refs_6_.refs_17_ = bf16[520,384]{1,0:T(8,128)(2,1)S(1)} collective-permute-done((bf16[520,384]{1,0:T(8,128)(2,1)S(1)}, bf16[520,384]{1,0:T(8,128)(2,1)S(1)}, u32[]{:S(2)}, u32[]{:S(2)}) %collective-permute-start.30) | collective-permute-done | bytes 399392 | tf_op jit(solution)/shard_map/ppermute | solution.py:395
  120.4 7.0 %collective-permute-done.7.refs_7_ = bf16[64,4096]{1,0:T(8,128)(2,1)S(1)} collective-permute-done((bf16[64,4096]{1,0:T(8,128)(2,1)S(1)}, bf16[64,4096]{1,0:T(8,128)(2,1)S(1)}, u32[]{:S(2)}, u32[]{:S(2)}) %collective-permute-start.7) | collective-permute-done | bytes 524320 | tf_op jit(solution)/shard_map/ppermute | solution.py:343
  127.4 10.0 %collective-permute-done.8.refs_8_ = bf16[64,4096]{1,0:T(8,128)(2,1)S(1)} collective-permute-done((bf16[64,4096]{1,0:T(8,128)(2,1)S(1)}, bf16[64,4096]{1,0:T(8,128)(2,1)S(1)}, u32[]{:S(2)}, u32[]{:S(2)}) %collective-permute-start.8) | collective-permute-done | bytes 524320 | tf_op jit(solution)/shard_map/ppermute | solution.py:343
  137.4 6.1 %shard_map.86.tok_ref.refs_0_ = bf16[768,4096]{1,0:T(8,128)(2,1)} custom-call(s32[4]{0:T(128)S(1)} %copy-done.8, bf16[768,4096]{1,0:T(8,128)(2,1)} %tok_ref.3), custom_call_target="tpu_custom_call" | custom-call | flops 1000000 | bytes 12582912 | tf_op jit(solution)/shard_map/pallas_call | solution.py:71
  143.6 2.8 %copy-done = bf16[768,4096]{1,0:T(8,128)(2,1)S(1)} copy-done((bf16[768,4096]{1,0:T(8,128)(2,1)S(1)}, bf16[768,4096]{1,0:T(8,128)(2,1)}, u32[]{:S(2)}) %copy-start) | copy-done | bytes 6291480
  151.4 3.5 %shard_map.94.own_ref.refs_0_.refs_1_ = bf16[768,384]{1,0:T(8,128)(2,1)S(1)} custom-call(f32[8,128]{1,0:T(8,128)S(1)} %copy-done.4, bf16[768,4096]{1,0:T(8,128)(2,1)S(1)} %copy-done.1, bf16[520,384]{1,0:T(8,128)(2,1)S(1)} %copy-done.3, bf16[520,384]{1,0:T(8,128)(2,1)S(1)} %collective-permute-done.26.refs_1_.refs_2_.refs_13_, ...), custom_call_target="tpu_custom_call" | custom-call | flops 2415919104 | bytes 6291456 | tf_op jit(solution)/shard_map/pallas_call | solution.py:27
  155.0 3.8 %collective-permute-start.20 = (bf16[512,128]{1,0:T(8,128)(2,1)S(1)}, bf16[512,128]{1,0:T(8,128)(2,1)S(1)}, u32[]{:S(2)}, u32[]{:S(2)}) collective-permute-start(bf16[512,128]{1,0:T(8,128)(2,1)S(1)} %copy-done.9), channel_id=1, source_target_pairs={{8,0},{12,4},{16,8},{20,12},{24,16},{28,20},{0,24},{4,28},{9,1},{1... | collective-permute-start | bytes 393224 | tf_op jit(solution)/shard_map/ppermute | solution.py:392
  159.5 3.5 %shard_map.95.far_ref.refs_2_.refs_3_ = bf16[768,384]{1,0:T(8,128)(2,1)S(1)} custom-call(f32[8,128]{1,0:T(8,128)S(1)} %copy-done.4, bf16[64,4096]{1,0:T(8,128)(2,1)S(1)} %collective-permute-done.refs_0_, bf16[64,4096]{1,0:T(8,128)(2,1)S(1)} %collective-permute-done.1.refs_1_, bf16[64,4096]{1,0:T(8,128)(2,1)S(1)} %collective-permute-done.2.refs_2_, ...), custom_call_target="tpu_custom_call" | custom-call | flops 2415919104 | bytes 6291456 | tf_op jit(solution)/shard_map/pallas_call | solution.py:27
  162.9 3.3 %collective-permute-done.33.winp_ref.refs_2_.refs_5_ = f32[8,768]{1,0:T(8,128)S(1)} collective-permute-done((f32[8,768]{1,0:T(8,128)S(1)}, f32[8,768]{1,0:T(8,128)S(1)}, u32[]{:S(2)}, u32[]{:S(2)}) %collective-permute-start.33) | collective-permute-done | bytes 24608 | tf_op jit(solution)/shard_map/ppermute | solution.py:407
  176.6 5.1 %collective-permute-start.44 = (f32[128,128]{1,0:T(8,128)S(1)}, f32[128,128]{1,0:T(8,128)S(1)}, u32[]{:S(2)}, u32[]{:S(2)}) collective-permute-start(f32[128,128]{1,0:T(8,128)S(1)} %shard_map.97), channel_id=1, source_target_pairs={{0,16},{4,20},{8,24},{12,28},{1,17},{5,21},{9,25},{13,29},{2,18},{... | collective-permute-start | bytes 196616 | tf_op jit(solution)/shard_map/ppermute | solution.py:456
  181.8 2.7 %collective-permute-start.35 = (f32[128,128]{1,0:T(8,128)S(1)}, f32[128,128]{1,0:T(8,128)S(1)}, u32[]{:S(2)}, u32[]{:S(2)}) collective-permute-start(f32[128,128]{1,0:T(8,128)S(1)} %shard_map.90), channel_id=1, source_target_pairs={{0,16},{4,20},{8,24},{12,28},{1,17},{5,21},{9,25},{13,29},{2,18},{... | collective-permute-start | bytes 196616 | tf_op jit(solution)/shard_map/ppermute | solution.py:456
  203.9 4.2 %collective-permute-done.46.refs_2_ = bf16[768,128]{1,0:T(8,128)(2,1)S(1)} collective-permute-done((bf16[768,128]{1,0:T(8,128)(2,1)S(1)}, bf16[768,128]{1,0:T(8,128)(2,1)S(1)}, u32[]{:S(2)}, u32[]{:S(2)}) %collective-permute-start.46) | collective-permute-done | bytes 196640 | tf_op jit(solution)/shard_map/ppermute | solution.py:343
  208.2 3.3 %collective-permute-done.50.refs_6_ = bf16[768,128]{1,0:T(8,128)(2,1)S(1)} collective-permute-done((bf16[768,128]{1,0:T(8,128)(2,1)S(1)}, bf16[768,128]{1,0:T(8,128)(2,1)S(1)}, u32[]{:S(2)}, u32[]{:S(2)}) %collective-permute-start.50) | collective-permute-done | bytes 196640 | tf_op jit(solution)/shard_map/ppermute | solution.py:343
  (128 shorter events, 73.0 us)
Async XLA Ops:
  6.5 53.2 %collective-permute-start.31 = (bf16[520,384]{1,0:T(8,128)(2,1)}, bf16[520,384]{1,0:T(8,128)(2,1)S(1)}, u32[]{:S(2)}, u32[]{:S(2)}) collective-permute-start(bf16[520,384]{1,0:T(8,128)(2,1)} %get-tuple-element.24), channel_id=1, source_target_pairs={{24,0},{28,4},{0,8},{4,12},{8,16},{12,20},{16,24},{20,28},{25,1},{... | collective-permute-start | bytes 1198088 | tf_op jit(solution)/shard_map/ppermute | solution.py:392
  8.1 21.2 %collective-permute-start.13 = (bf16[512,256]{1,0:T(8,128)(2,1)}, bf16[512,256]{1,0:T(8,128)(2,1)S(1)}, u32[]{:S(2)}, u32[]{:S(2)}) collective-permute-start(bf16[512,256]{1,0:T(8,128)(2,1)} %get-tuple-element.20), channel_id=1, source_target_pairs={{8,0},{12,4},{16,8},{20,12},{24,16},{28,20},{0,24},{4,28},{9,1},{1... | collective-permute-start | bytes 786440 | tf_op jit(solution)/shard_map/ppermute | solution.py:392
  10.3 49.4 %collective-permute-start.27 = (bf16[520,384]{1,0:T(8,128)(2,1)}, bf16[520,384]{1,0:T(8,128)(2,1)S(1)}, u32[]{:S(2)}, u32[]{:S(2)}) collective-permute-start(bf16[520,384]{1,0:T(8,128)(2,1)} %get-tuple-element.24), channel_id=1, source_target_pairs={{8,0},{12,4},{16,8},{20,12},{24,16},{28,20},{0,24},{4,28},{9,1},{1... | collective-permute-start | bytes 1198088 | tf_op jit(solution)/shard_map/ppermute | solution.py:392
  10.6 47.0 %collective-permute-start.15 = (bf16[512,256]{1,0:T(8,128)(2,1)}, bf16[512,256]{1,0:T(8,128)(2,1)S(1)}, u32[]{:S(2)}, u32[]{:S(2)}) collective-permute-start(bf16[512,256]{1,0:T(8,128)(2,1)} %get-tuple-element.19.refs_12_.refs_1_), channel_id=1, source_target_pairs={{16,0},{20,4},{24,8},{28,12},{0,16},{4,20},{8,24},{12,28},{17,1},{... | collective-permute-start | bytes 786440 | tf_op jit(solution)/shard_map/ppermute | solution.py:392
  16.0 41.7 %collective-permute-start.12 = (bf16[512,256]{1,0:T(8,128)(2,1)}, bf16[512,256]{1,0:T(8,128)(2,1)S(1)}, u32[]{:S(2)}, u32[]{:S(2)}) collective-permute-start(bf16[512,256]{1,0:T(8,128)(2,1)} %get-tuple-element.19.refs_12_.refs_1_), channel_id=1, source_target_pairs={{0,4},{4,0},{8,12},{12,8},{16,20},{20,16},{24,28},{28,24},{1,5},{5... | collective-permute-start | bytes 786440 | tf_op jit(solution)/shard_map/ppermute | solution.py:395
  29.3 36.9 %collective-permute-start.29 = (bf16[520,384]{1,0:T(8,128)(2,1)}, bf16[520,384]{1,0:T(8,128)(2,1)S(1)}, u32[]{:S(2)}, u32[]{:S(2)}) collective-permute-start(bf16[520,384]{1,0:T(8,128)(2,1)} %get-tuple-element.23.refs_0_.refs_1_.refs_12_), channel_id=1, source_target_pairs={{16,0},{20,4},{24,8},{28,12},{0,16},{4,20},{8,24},{12,28},{17,1},{... | collective-permute-start | bytes 1198088 | tf_op jit(solution)/shard_map/ppermute | solution.py:392
  57.6 19.8 %collective-permute-start = (bf16[64,4096]{1,0:T(8,128)(2,1)}, bf16[64,4096]{1,0:T(8,128)(2,1)S(1)}, u32[]{:S(2)}, u32[]{:S(2)}) collective-permute-start(bf16[64,4096]{1,0:T(8,128)(2,1)} %get-tuple-element.16), channel_id=1, source_target_pairs={{0,8},{4,12},{8,0},{12,4},{16,24},{20,28},{24,16},{28,20},{1,9},{5... | collective-permute-start | bytes 1572872 | tf_op jit(solution)/shard_map/ppermute | solution.py:370
  57.6 31.0 %collective-permute-start.1 = (bf16[64,4096]{1,0:T(8,128)(2,1)}, bf16[64,4096]{1,0:T(8,128)(2,1)S(1)}, u32[]{:S(2)}, u32[]{:S(2)}) collective-permute-start(bf16[64,4096]{1,0:T(8,128)(2,1)} %get-tuple-element.17), channel_id=1, source_target_pairs={{0,8},{4,12},{8,0},{12,4},{16,24},{20,28},{24,16},{28,20},{1,9},{5... | collective-permute-start | bytes 1572872 | tf_op jit(solution)/shard_map/ppermute | solution.py:370
  59.7 40.1 %collective-permute-start.2 = (bf16[64,4096]{1,0:T(8,128)(2,1)}, bf16[64,4096]{1,0:T(8,128)(2,1)S(1)}, u32[]{:S(2)}, u32[]{:S(2)}) collective-permute-start(bf16[64,4096]{1,0:T(8,128)(2,1)} %get-tuple-element.18), channel_id=1, source_target_pairs={{0,8},{4,12},{8,0},{12,4},{16,24},{20,28},{24,16},{28,20},{1,9},{5... | collective-permute-start | bytes 1572872 | tf_op jit(solution)/shard_map/ppermute | solution.py:370
  66.2 43.3 %collective-permute-start.32 = (bf16[520,384]{1,0:T(8,128)(2,1)S(1)}, bf16[520,384]{1,0:T(8,128)(2,1)S(1)}, u32[]{:S(2)}, u32[]{:S(2)}) collective-permute-start(bf16[520,384]{1,0:T(8,128)(2,1)S(1)} %collective-permute-done.31.refs_6_.refs_7_.refs_18_), channel_id=1, source_target_pairs={{0,4},{4,0},{8,12},{12,8},{16,20},{20,16},{24,28},{28,24},{1,5},{5... | collective-permute-start | bytes 1198088 | tf_op jit(solution)/shard_map/ppermute | solution.py:395
  71.8 38.3 %collective-permute-start.28 = (bf16[520,384]{1,0:T(8,128)(2,1)S(1)}, bf16[520,384]{1,0:T(8,128)(2,1)S(1)}, u32[]{:S(2)}, u32[]{:S(2)}) collective-permute-start(bf16[520,384]{1,0:T(8,128)(2,1)S(1)} %collective-permute-done.27.refs_2_.refs_3_.refs_14_), channel_id=1, source_target_pairs={{0,4},{4,0},{8,12},{12,8},{16,20},{20,16},{24,28},{28,24},{1,5},{5... | collective-permute-start | bytes 1198088 | tf_op jit(solution)/shard_map/ppermute | solution.py:395
  77.4 23.9 %collective-permute-start.18 = (bf16[512,256]{1,0:T(8,128)(2,1)S(1)}, bf16[512,256]{1,0:T(8,128)(2,1)S(1)}, u32[]{:S(2)}, u32[]{:S(2)}) collective-permute-start(bf16[512,256]{1,0:T(8,128)(2,1)S(1)} %collective-permute-done.17.refs_18_.refs_7_), channel_id=1, source_target_pairs={{0,4},{4,0},{8,12},{12,8},{16,20},{20,16},{24,28},{28,24},{1,5},{5... | collective-permute-start | bytes 786440 | tf_op jit(solution)/shard_map/ppermute | solution.py:395
  101.3 18.5 %collective-permute-start.6 = (bf16[64,4096]{1,0:T(8,128)(2,1)S(1)}, bf16[64,4096]{1,0:T(8,128)(2,1)S(1)}, u32[]{:S(2)}, u32[]{:S(2)}) collective-permute-start(bf16[64,4096]{1,0:T(8,128)(2,1)S(1)} %collective-permute-done.refs_0_), channel_id=1, source_target_pairs={{0,2},{1,3},{2,0},{3,1},{4,6},{5,7},{6,4},{7,5},{8,10},{9,11},{10,... | collective-permute-start | bytes 1572872 | tf_op jit(solution)/shard_map/ppermute | solution.py:343
  102.8 17.5 %collective-permute-start.3 = (bf16[64,4096]{1,0:T(8,128)(2,1)S(1)}, bf16[64,4096]{1,0:T(8,128)(2,1)S(1)}, u32[]{:S(2)}, u32[]{:S(2)}) collective-permute-start(bf16[64,4096]{1,0:T(8,128)(2,1)S(1)} %collective-permute-done.refs_0_), channel_id=1, source_target_pairs={{0,1},{1,0},{2,3},{3,2},{4,5},{5,4},{6,7},{7,6},{8,9},{9,8},{10,11... | collective-permute-start | bytes 1572872 | tf_op jit(solution)/shard_map/ppermute | solution.py:343
  108.0 19.3 %collective-permute-start.7 = (bf16[64,4096]{1,0:T(8,128)(2,1)S(1)}, bf16[64,4096]{1,0:T(8,128)(2,1)S(1)}, u32[]{:S(2)}, u32[]{:S(2)}) collective-permute-start(bf16[64,4096]{1,0:T(8,128)(2,1)S(1)} %collective-permute-done.1.refs_1_), channel_id=1, source_target_pairs={{0,2},{1,3},{2,0},{3,1},{4,6},{5,7},{6,4},{7,5},{8,10},{9,11},{10,... | collective-permute-start | bytes 1572872 | tf_op jit(solution)/shard_map/ppermute | solution.py:343
  109.5 27.8 %collective-permute-start.8 = (bf16[64,4096]{1,0:T(8,128)(2,1)S(1)}, bf16[64,4096]{1,0:T(8,128)(2,1)S(1)}, u32[]{:S(2)}, u32[]{:S(2)}) collective-permute-start(bf16[64,4096]{1,0:T(8,128)(2,1)S(1)} %collective-permute-done.2.refs_2_), channel_id=1, source_target_pairs={{0,2},{1,3},{2,0},{3,1},{4,6},{5,7},{6,4},{7,5},{8,10},{9,11},{10,... | collective-permute-start | bytes 1572872 | tf_op jit(solution)/shard_map/ppermute | solution.py:343
  119.8 35.1 %collective-permute-start.4 = (bf16[64,4096]{1,0:T(8,128)(2,1)S(1)}, bf16[64,4096]{1,0:T(8,128)(2,1)S(1)}, u32[]{:S(2)}, u32[]{:S(2)}) collective-permute-start(bf16[64,4096]{1,0:T(8,128)(2,1)S(1)} %collective-permute-done.1.refs_1_), channel_id=1, source_target_pairs={{0,1},{1,0},{2,3},{3,2},{4,5},{5,4},{6,7},{7,6},{8,9},{9,8},{10,11... | collective-permute-start | bytes 1572872 | tf_op jit(solution)/shard_map/ppermute | solution.py:343
  119.8 35.2 %collective-permute-start.5 = (bf16[64,4096]{1,0:T(8,128)(2,1)S(1)}, bf16[64,4096]{1,0:T(8,128)(2,1)S(1)}, u32[]{:S(2)}, u32[]{:S(2)}) collective-permute-start(bf16[64,4096]{1,0:T(8,128)(2,1)S(1)} %collective-permute-done.2.refs_2_), channel_id=1, source_target_pairs={{0,1},{1,0},{2,3},{3,2},{4,5},{5,4},{6,7},{7,6},{8,9},{9,8},{10,11... | collective-permute-start | bytes 1572872 | tf_op jit(solution)/shard_map/ppermute | solution.py:343
  120.3 38.5 %collective-permute-start.9 = (bf16[64,4096]{1,0:T(8,128)(2,1)S(1)}, bf16[64,4096]{1,0:T(8,128)(2,1)S(1)}, u32[]{:S(2)}, u32[]{:S(2)}) collective-permute-start(bf16[64,4096]{1,0:T(8,128)(2,1)S(1)} %collective-permute-done.6.refs_6_), channel_id=1, source_target_pairs={{0,1},{1,0},{2,3},{3,2},{4,5},{5,4},{6,7},{7,6},{8,9},{9,8},{10,11... | collective-permute-start | bytes 1572872 | tf_op jit(solution)/shard_map/ppermute | solution.py:343
  127.4 31.5 %collective-permute-start.10 = (bf16[64,4096]{1,0:T(8,128)(2,1)S(1)}, bf16[64,4096]{1,0:T(8,128)(2,1)S(1)}, u32[]{:S(2)}, u32[]{:S(2)}) collective-permute-start(bf16[64,4096]{1,0:T(8,128)(2,1)S(1)} %collective-permute-done.7.refs_7_), channel_id=1, source_target_pairs={{0,1},{1,0},{2,3},{3,2},{4,5},{5,4},{6,7},{7,6},{8,9},{9,8},{10,11... | collective-permute-start | bytes 1572872 | tf_op jit(solution)/shard_map/ppermute | solution.py:343
  137.4 22.1 %collective-permute-start.11 = (bf16[64,4096]{1,0:T(8,128)(2,1)S(1)}, bf16[64,4096]{1,0:T(8,128)(2,1)S(1)}, u32[]{:S(2)}, u32[]{:S(2)}) collective-permute-start(bf16[64,4096]{1,0:T(8,128)(2,1)S(1)} %collective-permute-done.8.refs_8_), channel_id=1, source_target_pairs={{0,1},{1,0},{2,3},{3,2},{4,5},{5,4},{6,7},{7,6},{8,9},{9,8},{10,11... | collective-permute-start | bytes 1572872 | tf_op jit(solution)/shard_map/ppermute | solution.py:343
  154.9 16.6 %collective-permute-start.24 = (bf16[512,128]{1,0:T(8,128)(2,1)S(1)}, bf16[512,128]{1,0:T(8,128)(2,1)S(1)}, u32[]{:S(2)}, u32[]{:S(2)}) collective-permute-start(bf16[512,128]{1,0:T(8,128)(2,1)S(1)} %copy-done.9), channel_id=1, source_target_pairs={{24,0},{28,4},{0,8},{4,12},{8,16},{12,20},{16,24},{20,28},{25,1},{... | collective-permute-start | bytes 393224 | tf_op jit(solution)/shard_map/ppermute | solution.py:392
  155.0 17.1 %collective-permute-start.20 = (bf16[512,128]{1,0:T(8,128)(2,1)S(1)}, bf16[512,128]{1,0:T(8,128)(2,1)S(1)}, u32[]{:S(2)}, u32[]{:S(2)}) collective-permute-start(bf16[512,128]{1,0:T(8,128)(2,1)S(1)} %copy-done.9), channel_id=1, source_target_pairs={{8,0},{12,4},{16,8},{20,12},{24,16},{28,20},{0,24},{4,28},{9,1},{1... | collective-permute-start | bytes 393224 | tf_op jit(solution)/shard_map/ppermute | solution.py:392
  158.8 14.8 %collective-permute-start.22 = (bf16[512,128]{1,0:T(8,128)(2,1)S(1)}, bf16[512,128]{1,0:T(8,128)(2,1)S(1)}, u32[]{:S(2)}, u32[]{:S(2)}) collective-permute-start(bf16[512,128]{1,0:T(8,128)(2,1)S(1)} %copy-done.6), channel_id=1, source_target_pairs={{16,0},{20,4},{24,8},{28,12},{0,16},{4,20},{8,24},{12,28},{17,1},{... | collective-permute-start | bytes 393224 | tf_op jit(solution)/shard_map/ppermute | solution.py:392
  (39 other events, 619.7 us)
